TPU v7x, 256 devices: a whole 4x4x8 slice. The times are simulated.
256 devices in a mesh: row: 16 (over x_hi, z), col: 16 (over x_lo, y, core).
Axes of the slice: x: 4 (x_hi: 2, x_lo: 2; x = x_hi * 2 + x_lo), y: 4, z: 8, core: 2. Of those that a mesh axis runs over, the one named last changes fastest.
Arguments:
- pair: bfloat16 [512, 512, 128], P('row', 'col'), may hold values from -6 to 6
- norm_in: float32 [128], replicated, may hold values from 0.1 to 1.9
- shift_in: float32 [128], replicated, may hold values from -3 to 3
- in_weight: bfloat16 [128, 640], replicated, may hold values from -0.5 to 0.5
- norm_out: float32 [128], replicated, may hold values from 0.1 to 1.9
- shift_out: float32 [128], replicated, may hold values from -3 to 3
- out_weight: bfloat16 [128, 128], replicated, may hold values from -0.5 to 0.5
Outputs:
- update: bfloat16 [512, 512, 128], P('row', 'col')
All inputs are finite; a program needn't handle non-finite values.
Results may differ from a plain program's by a relative error of at most 0.0054.
Values may be sent and summed in bfloat16 or wider, within the bound.
No kernel may reach another device: no remote copies, remote signals or barrier semaphores. Data moves between devices by JAX's collectives and lax.ppermute only.
A program may use at most 64 MiB of HBM per device.

v0:
```python
import jax
import jax.numpy as jnp
from jax import lax
from jax.sharding import PartitionSpec as P

EPSILON = 1e-05


def layer_norm(values, gain, shift):
    values = values.astype(jnp.float32)
    center = jnp.mean(values, axis=-1, keepdims=True)
    spread = jnp.mean(jnp.square(values - center), axis=-1, keepdims=True)
    return (values - center) * lax.rsqrt(spread + EPSILON) * gain + shift


def local(pair, norm_in, shift_in, in_weight, norm_out, shift_out, out_weight):
    row_count, col_count, channels = pair.shape
    hidden = out_weight.shape[0]
    normed = layer_norm(pair, norm_in, shift_in).astype(jnp.bfloat16)
    projected = jnp.dot(normed.reshape(-1, channels), in_weight, preferred_element_type=jnp.float32)
    left = (jax.nn.sigmoid(projected[:, :hidden]) * projected[:, hidden : 2 * hidden]).astype(
        jnp.bfloat16
    )
    right = (
        jax.nn.sigmoid(projected[:, 2 * hidden : 3 * hidden])
        * projected[:, 3 * hidden : 4 * hidden]
    ).astype(jnp.bfloat16)
    gate = jax.nn.sigmoid(projected[:, 4 * hidden :]).reshape(row_count, col_count, channels)
    left = left.reshape(row_count, col_count, hidden)
    right = right.reshape(row_count, col_count, hidden)
    row_devices = lax.axis_size("row")
    col_devices = lax.axis_size("col")
    unit = row_count // col_devices
    groups = row_devices // col_devices
    sectioned = left.reshape(row_count, groups, col_devices, unit, hidden).transpose(0, 2, 1, 3, 4)
    sorted_parts = lax.all_to_all(sectioned, "col", split_axis=1, concat_axis=1, tiled=True)
    sorted_parts = sorted_parts.reshape(row_count, row_devices, unit * hidden)
    own_parts = lax.all_to_all(sorted_parts, "row", split_axis=1, concat_axis=0, tiled=True)
    own_parts = own_parts.reshape(row_count * row_devices, unit, hidden)
    right_full = lax.all_gather(right, "row", axis=0, tiled=True)
    mixed = jnp.einsum(
        "kih,kjh->ijh",
        lax.all_gather(own_parts, "col", axis=1, tiled=True),
        right_full,
        preferred_element_type=jnp.float32,
    )
    mixed_normed = layer_norm(mixed, norm_out, shift_out).astype(jnp.bfloat16)
    outward = jnp.dot(
        mixed_normed.reshape(-1, hidden), out_weight, preferred_element_type=jnp.float32
    )
    return (gate * outward.reshape(row_count, col_count, channels)).astype(jnp.bfloat16)


def solution(mesh):
    in_specs = (P("row", "col", None), P(), P(), P(), P(), P(), P())
    out_specs = P("row", "col", None)
    return jax.shard_map(local, mesh=mesh, in_specs=in_specs, out_specs=out_specs, check_vma=False)
```

profile of v0, /device:TPU:1, one launch (start us, length us, event | category | flops | bytes accessed | tf_op | source)
XLA Modules:
  0.0 179.2 jit_solution(12223654991282901006)
XLA Ops:
  6.5 0.0 copy-start
  6.5 0.0 all-gather.3.cloned.1.call-start
  6.5 1.2 convert_reduce_fusion
  7.8 1.3 fusion.3
  9.1 1.3 fusion.6
  10.4 0.0 copy-done
  10.4 0.5 fusion.23
  10.9 1.1 fusion.7
  12.0 0.0 all-gather.3.cloned.1.call-update
  12.1 0.0 all-gather.5.cloned.1.call-start
  12.1 0.2 copy.34
  12.4 13.9 %all_to_all.20 = bf16[32,16,1,2,128]{4,3,0,2,1:T(2,128)(2,1)S(1)} all-to-all(bf16[32,16,1,2,128]{4,3,0,2,1:T(2,128)(2,1)S(1)} %copy.34), channel_id=1, replica_groups=mesh['row'=16,'col'=16] {'col'}, dimensions={1} | all-to-all | bytes 524288 | tf_op jit(solution)/shard_map/all_to_all | solution.py:36
  26.2 0.2 reshape.51
  26.4 24.2 %all_to_all.21 = bf16[32,16,256]{2,0,1:T(8,128)(2,1)S(1)} all-to-all(bf16[32,16,256]{2,0,1:T(8,128)(2,1)S(1)} %reshape.51), channel_id=1, replica_groups=mesh['row'=16,'col'=16] {'row'}, dimensions={1} | all-to-all | bytes 524288 | tf_op jit(solution)/shard_map/all_to_all | solution.py:38
  50.6 0.1 reshape.52
  50.7 0.7 copy.35
  51.4 0.0 all-gather.5.cloned.1.call-update
  51.5 62.9 %all-gather.3.cloned.1.call-done = bf16[512,32,128]{2,1,0:T(8,128)(2,1)} async-done(((bf16[32,32,128]{2,1,0:T(8,128)(2,1)}), bf16[512,32,128]{2,1,0:T(8,128)(2,1)}) %all-gather.3.cloned.1.call-update) | async-done | bytes 4194320 | tf_op jit(solution)/shard_map/all_gather | solution.py:40
  114.4 8.6 %copy.36 = bf16[512,32,128]{0,1,2:T(8,128)(2,1)} copy(bf16[512,32,128]{2,1,0:T(8,128)(2,1)} %all-gather.3.cloned.1.call-done) | data formatting | bytes 8388608 | tf_op jit(solution)/shard_map/all_gather | solution.py:40
  123.0 33.6 %all-gather.5.cloned.1.call-done = bf16[512,32,128]{2,0,1:T(8,128)(2,1)} async-done(((bf16[512,2,128]{2,0,1:T(8,128)(2,1)}), bf16[512,32,128]{2,0,1:T(8,128)(2,1)}) %all-gather.5.cloned.1.call-update) | async-done | bytes 4194320 | tf_op jit(solution)/shard_map/all_gather | solution.py:43
  156.6 7.9 %copy.37 = bf16[512,32,128]{0,1,2:T(8,128)(2,1)} copy(bf16[512,32,128]{2,0,1:T(8,128)(2,1)} %all-gather.5.cloned.1.call-done) | data formatting | bytes 8388608 | tf_op jit(solution)/shard_map/all_gather | solution.py:43
  164.5 0.0 copy-start.1
  164.5 0.0 copy-start.2
  164.5 0.0 copy-start.3
  164.5 4.7 %bitcast_reduce_fusion = (f32[32,32]{0,1:T(8,128)S(1)}, f32[128,32,32]{2,1,0:T(8,128)S(1)}) fusion(bf16[512,32,128]{0,1,2:T(8,128)(2,1)} %copy.36, bf16[512,32,128]{0,1,2:T(8,128)(2,1)} %copy.37), kind=kOutput, calls=%fused_computation | convolution fusion | flops 134347776 | bytes 8916992 | tf_op jit(solution)/shard_map/kih,kjh->ijh/dot_general | solution.py:41
  169.2 0.1 copy.40
  169.3 1.4 copy.38
  170.8 0.4 multiply_reduce_fusion
  171.2 0.0 copy-done.1
  171.2 0.0 copy-done.2
  171.2 0.0 copy-done.3
  171.2 1.2 fusion
  (4 shorter events, 0.0 us)
Async XLA Ops:
  6.5 3.9 %copy-start = (bf16[128,640]{1,0:T(8,128)(2,1)S(1)}, bf16[128,640]{1,0:T(8,128)(2,1)}, u32[]{:S(2)}) copy-start(bf16[128,640]{1,0:T(8,128)(2,1)} %param.10) | copy-start | bytes 491524
  6.5 107.9 %all-gather.3.cloned.1.call-start = ((), (), s32[]{:S(2)}) async-start(), calls=%async_computation.2 | async-start | bytes 4456448 | tf_op jit(solution)/shard_map/all_gather | solution.py:40
  12.1 144.5 %all-gather.5.cloned.1.call-start = ((), (), s32[]{:S(2)}) async-start(), calls=%async_computation.3 | async-start | bytes 4456448 | tf_op jit(solution)/shard_map/all_gather | solution.py:43
  164.5 6.6 %copy-start.1 = (bf16[128,128]{1,0:T(8,128)(2,1)S(1)}, bf16[128,128]{1,0:T(8,128)(2,1)}, u32[]{:S(2)}) copy-start(bf16[128,128]{1,0:T(8,128)(2,1)} %param.13) | copy-start | bytes 98308
  164.5 6.7 %copy-start.2 = (f32[128]{0:T(128)S(1)}, f32[128]{0:T(128)}, u32[]{:S(2)}) copy-start(f32[128]{0:T(128)} %param.12) | copy-start | bytes 1540
  164.5 6.7 %copy-start.3 = (f32[128]{0:T(128)S(1)}, f32[128]{0:T(128)}, u32[]{:S(2)}) copy-start(f32[128]{0:T(128)} %param.11) | copy-start | bytes 1540
Sparse Core Ops, SparseCore 0:
  12.2 102.1 all-gather.2
  116.2 40.3 all-gather.4
where the time goes:
time: 180 us; the launch traced here: 179 us
  waiting for transfers between devices  96.5 us (54%)
  blocking collectives  38.1 us (21%)
  local copies, waits for them, and re-layouts  19.3 us (11%)
  between operations  13.5 us (8%)
  matrix products  6.37 us (4%)
  other arithmetic  5.36 us (3%)
    all_gather x1, waiting for transfers between devices, local(): right_full = lax.all_gather(right, 'row', axis=0, tiled=True)  62.9 us
    all_gather x1, waiting for transfers between devices, local(): lax.all_gather(own_parts, 'col', axis=1, tiled=True)  33.6 us
    all_to_all x1, blocking collectives, local(): lax.all_to_all(sorted_parts, 'row', split_axis=1, concat_axis=0, tiled=True)  24.2 us
    all_to_all x1, blocking collectives, local(): lax.all_to_all(sectioned, 'col', split_axis=1, concat_axis=1, tiled=True)  13.9 us
    all_gather x1, local copies, waits for them, and re-layouts, local(): right_full = lax.all_gather(right, 'row', axis=0, tiled=True)  8.62 us
    all_gather x1, local copies, waits for them, and re-layouts, local(): lax.all_gather(own_parts, 'col', axis=1, tiled=True)  7.93 us
    dot_general x1, matrix products, local(): jnp.einsum('kih,kjh->ijh', lax.all_gather(own_parts, 'col', axis=1, tiled...  4.72 us
  transfers between devices with their start and end apart: 2, of which 2 were waited for; matrix products, arithmetic and copies ran while one was open for 5% of the time, Pallas kernels for 0%

commit v1 on v0

v1 whole, which is shorter than its diff:
```python
import jax
import jax.numpy as jnp
from jax import lax
from jax.experimental import pallas as pl
from jax.experimental.pallas import tpu as pltpu
from jax.sharding import Mesh, PartitionSpec as P

EPSILON = 1e-05
CHIPS = ("xh", "z", "xl", "y")
F32 = jnp.float32
BF16 = jnp.bfloat16
VMEM = pl.BlockSpec(memory_space=pltpu.VMEM)
SMEM = pl.BlockSpec(memory_space=pltpu.SMEM)


def swap_groups(v):
    lane = lax.broadcasted_iota(jnp.int32, v[0].shape, 1)
    low = lane < 64
    u = [None] * 4
    for c in (0, 1):
        a, b = v[c], v[c + 2]
        u[c] = jnp.where(low, a, pltpu.roll(b, 64, 1))
        u[c + 2] = jnp.where(low, pltpu.roll(a, 64, 1), b)
    even = (lane & 32) == 0
    out = [None] * 4
    for c in (0, 2):
        a, b = u[c], u[c + 1]
        out[c] = jnp.where(even, a, pltpu.roll(b, 32, 1))
        out[c + 1] = jnp.where(even, pltpu.roll(a, 96, 1), b)
    return out


def project_kernel(pair_ref, gain_ref, shift_ref, w_ref, msg_ref, normed_ref, scr_ref):
    gain = gain_ref[...]
    shift = shift_ref[...]
    wt = jnp.transpose(w_ref[:, :512].astype(F32)).astype(BF16)
    for a in range(8):
        x = pair_ref[a * 128 : (a + 1) * 128, :].astype(F32)
        center = jnp.mean(x, axis=-1, keepdims=True)
        d = x - center
        spread = jnp.mean(d * d, axis=-1, keepdims=True)
        n = (d * lax.rsqrt(spread + EPSILON) * gain + shift).astype(BF16)
        normed_ref[a * 128 : (a + 1) * 128, :] = n
        p = lax.dot_general(wt, n, (((1,), (1,)), ((), ())), preferred_element_type=F32)
        left = jax.nn.sigmoid(p[0:128]) * p[128:256]
        right = jax.nn.sigmoid(p[256:384]) * p[384:512]
        scr_ref[pl.ds(a, 128, stride=16), :] = left
        scr_ref[pl.ds(8 + a, 128, stride=16), :] = right
    msg_ref[...] = scr_ref[...].astype(BF16)


def gate_kernel(normed_ref, w_ref, gate_ref):
    gate_ref[...] = jax.nn.sigmoid(
        jnp.dot(normed_ref[...], w_ref[:, 512:640], preferred_element_type=F32)
    )


def spread_kernel(offset, recv_ref, out_ref):
    for r in range(16):
        for g in range(2):
            base = (r * 8 + g * 4) * 16
            v = [
                recv_ref[base + c * 16 : base + c * 16 + 16, :].astype(F32)[offset : offset + 8]
                for c in range(4)
            ]
            out_ref[r * 32 : (r + 1) * 32, g * 128 : (g + 1) * 128] = jnp.concatenate(
                swap_groups(v), axis=0
            ).astype(BF16)


def mix_kernel(core_ref, own_ref, other_ref, right_ref, out_ref):
    core = core_ref[0]
    right = right_ref[...]
    for part, ref in ((core, own_ref), (1 - core, other_ref)):
        mixed = lax.dot_general(
            ref[...], right, (((0,), (0,)), ((), ())), preferred_element_type=F32
        )
        for q in range(8):
            row = 2 * q + part
            for g in range(2):
                v = mixed[q * 32 : (q + 1) * 32, g * 128 : (g + 1) * 128]
                v = [v[b * 8 : (b + 1) * 8] for b in range(4)]
                start = pl.multiple_of(row * 64 + g * 32, 32)
                out_ref[pl.ds(start, 32), :] = jnp.concatenate(swap_groups(v), axis=0).astype(BF16)


def output_kernel(recv_ref, gate_ref, gain_ref, shift_ref, w_ref, out_ref, scr_ref):
    total = jnp.zeros((8, 128), F32)
    for t in range(64):
        x = recv_ref[t * 16 : (t + 1) * 16, :].astype(F32)
        total = total + x[0:8] + x[8:16]
    center = total * (1.0 / 128.0)
    square = jnp.zeros((8, 128), F32)
    for t in range(64):
        x = recv_ref[t * 16 : (t + 1) * 16, :].astype(F32)
        d0 = x[0:8] - center
        d1 = x[8:16] - center
        square = square + d0 * d0 + d1 * d1
    scale = lax.rsqrt(square * (1.0 / 128.0) + EPSILON)
    for t in range(64):
        x = recv_ref[t * 16 : (t + 1) * 16, :].astype(F32)
        for k in range(2):
            h = 2 * t + k
            scr_ref[h * 8 : (h + 1) * 8, :] = (x[k * 8 : k * 8 + 8] - center) * scale * gain_ref[
                h
            ] + shift_ref[h]
    w = w_ref[...]
    for s in range(8):
        x = scr_ref[pl.ds(s, 128, stride=8), :].astype(BF16)
        o = lax.dot_general(x, w, (((0,), (0,)), ((), ())), preferred_element_type=F32)
        for b in range(4):
            i = b * 8 + s
            rows = slice(i * 32, (i + 1) * 32)
            out_ref[rows, :] = (gate_ref[rows, :] * o[b * 32 : (b + 1) * 32]).astype(BF16)


def local(pair, norm_in, shift_in, in_weight, norm_out, shift_out, out_weight):
    core = lax.axis_index("core").astype(jnp.int32).reshape(1)
    msg, normed = pl.pallas_call(
        project_kernel,
        out_shape=(
            jax.ShapeDtypeStruct((2048, 128), BF16),
            jax.ShapeDtypeStruct((1024, 128), BF16),
        ),
        in_specs=[VMEM] * 4,
        out_specs=(VMEM, VMEM),
        scratch_shapes=[pltpu.VMEM((2048, 128), F32)],
        name="project",
    )(pair.reshape(1024, 128), norm_in.reshape(1, 128), shift_in.reshape(1, 128), in_weight)
    recv = lax.all_to_all(msg.reshape(128, 16, 128), CHIPS, 0, 0, tiled=True).reshape(2048, 128)
    gate = pl.pallas_call(
        gate_kernel,
        out_shape=jax.ShapeDtypeStruct((1024, 128), F32),
        in_specs=[VMEM] * 2,
        out_specs=VMEM,
        name="gate",
        cost_estimate=pl.CostEstimate(flops=1 << 25, bytes_accessed=1 << 20, transcendentals=1 << 17),
    )(normed, in_weight)

    def spread(offset, name):
        return pl.pallas_call(
            lambda a, b: spread_kernel(offset, a, b),
            out_shape=jax.ShapeDtypeStruct((512, 256), BF16),
            in_specs=[VMEM],
            out_specs=VMEM,
            name=name,
            cost_estimate=pl.CostEstimate(flops=1 << 22, bytes_accessed=1 << 20, transcendentals=0),
        )(recv)

    own = spread(0, "spread_left")
    other = lax.ppermute(own, "core", [(0, 1), (1, 0)])
    right = spread(8, "spread_right")
    back = pl.pallas_call(
        mix_kernel,
        out_shape=jax.ShapeDtypeStruct((1024, 128), BF16),
        in_specs=[SMEM, VMEM, VMEM, VMEM],
        out_specs=VMEM,
        name="mix",
    )(core, own, other, right)
    mixed = lax.all_to_all(back.reshape(128, 8, 128), CHIPS, 0, 0, tiled=True).reshape(1024, 128)
    out = pl.pallas_call(
        output_kernel,
        out_shape=jax.ShapeDtypeStruct((1024, 128), BF16),
        in_specs=[VMEM, VMEM, SMEM, SMEM, VMEM],
        out_specs=VMEM,
        scratch_shapes=[pltpu.VMEM((1024, 128), F32)],
        name="output",
    )(mixed, gate, norm_out, shift_out, out_weight)
    return out.reshape(pair.shape)


def solution(mesh):
    fine = Mesh(mesh.devices.reshape(2, 8, 2, 4, 2), ("xh", "z", "xl", "y", "core"))
    spec = P(("xh", "z"), ("xl", "y", "core"), None)
    in_specs = (spec, P(), P(), P(), P(), P(), P())
    return jax.shard_map(local, mesh=fine, in_specs=in_specs, out_specs=spec, check_vma=False)
```

time: 180 us -> 73.6 us (0.41)
  waiting for transfers between devices: 96.5 us -> 12.9 us
  local copies, waits for them, and re-layouts: 19.3 us -> 1.39 us
  Pallas kernels: 0 us -> 14.8 us
  between operations: 13.5 us -> 0.02 us
  starting transfers between devices: 0.04 us -> 8.85 us
  matrix products: 6.37 us -> 0 us
  other arithmetic: 5.36 us -> 0 us
  blocking collectives: 38.1 us -> 35.4 us
    all_gather x2 -> x0, waiting for transfers between devices: 96.5 us -> none  [the longest x1 62.9 us: local(): right_full = lax.all_gather(right, 'row', axis=0, tiled=True)]
    all_gather x2 -> x0, local copies, waits for them, and re-layouts: 16.5 us -> none  [the longest x1 8.62 us: local(): right_full = lax.all_gather(right, 'row', axis=0, tiled=True)]
    pallas_call x0 -> x6, Pallas kernels: none -> 14.8 us  [the longest x2 4.87 us: spread(): pl.pallas_call(lambda a, b: spread_kernel(offset, a, b), out_shape=jax.Sh...]
    all_to_all x0 -> x1, waiting for transfers between devices: none -> 12.9 us  [local(): lax.all_to_all(back.reshape(128, 8, 128), CHIPS, 0, 0, tiled=True)]
    dot_general x3 -> x0, matrix products: 6.37 us -> none  [the longest x1 4.72 us: local(): jnp.einsum('kih,kjh->ijh', lax.all_gather(own_parts, 'col', axis=1, tiled...]
    all_to_all x0 -> x1, starting transfers between devices: none -> 6.16 us  [local(): lax.all_to_all(back.reshape(128, 8, 128), CHIPS, 0, 0, tiled=True)]
    reduce_sum x3 -> x0, other arithmetic: 2.9 us -> none  [the longest x2 1.71 us: layer_norm(): spread = jnp.mean(jnp.square(values - center), axis=-1, keepdims=True)]
    all_to_all x2 -> x1, blocking collectives: 38.1 us -> 35.4 us  [local(): lax.all_to_all(msg.reshape(128, 16, 128), CHIPS, 0, 0, tiled=True)]
  transfers between devices with their start and end apart: 2 -> 2, of which waited for: 2 -> 1; matrix products, arithmetic and copies ran while one was open for 5% -> 0% of each run, Pallas kernels for 0% -> 6%
where the time goes in v1:
time: 73.6 us; the launch traced here: 73.2 us
  blocking collectives  35.4 us (48%)
  Pallas kernels  14.8 us (20%)
  waiting for transfers between devices  12.9 us (18%)
  starting transfers between devices  8.85 us (12%)
  local copies, waits for them, and re-layouts  1.39 us (2%)
    all_to_all x1, blocking collectives, local(): lax.all_to_all(msg.reshape(128, 16, 128), CHIPS, 0, 0, tiled=True)  35.4 us
    all_to_all x1, waiting for transfers between devices, local(): lax.all_to_all(back.reshape(128, 8, 128), CHIPS, 0, 0, tiled=True)  12.9 us
    all_to_all x1, starting transfers between devices, local(): lax.all_to_all(back.reshape(128, 8, 128), CHIPS, 0, 0, tiled=True)  6.16 us
    pallas_call x2, Pallas kernels, spread(): pl.pallas_call(lambda a, b: spread_kernel(offset, a, b), out_shape=jax.Sh...  4.87 us
    pallas_call x1, Pallas kernels, local(): pl.pallas_call(project_kernel, out_shape=(jax.ShapeDtypeStruct((2048, 128...  3.06 us
    ppermute x1, starting transfers between devices, local(): other = lax.ppermute(own, 'core', [(0, 1), (1, 0)])  2.7 us
    pallas_call x1, Pallas kernels, local(): pl.pallas_call(output_kernel, out_shape=jax.ShapeDtypeStruct((1024, 128),...  2.49 us
    pallas_call x1, Pallas kernels, local(): pl.pallas_call(mix_kernel, out_shape=jax.ShapeDtypeStruct((1024, 128), BF...  2.34 us
  transfers between devices with their start and end apart: 2, of which 1 were waited for; matrix products, arithmetic and copies ran while one was open for 0% of the time, Pallas kernels for 6%

profile of v1, /device:TPU:1, one launch (start us, length us, event | category | flops | bytes accessed | tf_op | source)
XLA Modules:
  0.0 73.2 jit_solution(10141901688265929897)
XLA Ops:
  0.0 3.1 %project.1 = (bf16[2048,128]{1,0:T(8,128)(2,1)}, bf16[1024,128]{1,0:T(8,128)(2,1)}) custom-call(bf16[1024,128]{1,0:T(8,128)(2,1)} %bitcast.14, f32[1,128]{1,0:T(1,128)} %bitcast.15, f32[1,128]{1,0:T(1,128)} %bitcast.16, bf16[128,640]{1,0:T(8,128)(2,1)} %w_ref.4), custom_call_target="tpu_custom_call" | custom-call | tf_op jit(solution)/shard_map/project/pallas_call | solution.py:119
  3.1 35.4 %all_to_all.10 = bf16[128,16,128]{2,1,0:T(8,128)(2,1)} all-to-all(bf16[128,16,128]{2,1,0:T(8,128)(2,1)} %bitcast.13), channel_id=1, replica_groups=mesh['xh'=2,'z'=8,'xl'=2,'y'=4,'core'=2] {'xh','z','xl','y'}, dimensions={0} | all-to-all | bytes 1048576 | tf_op jit(solution)/shard_map/all_to_all | solution.py:130
  38.4 2.4 %spread_left.1.own_ref = bf16[512,256]{1,0:T(8,128)(2,1)} custom-call(bf16[2048,128]{1,0:T(8,128)(2,1)} %bitcast.9), custom_call_target="tpu_custom_call" | custom-call | flops 4194304 | bytes 1048576 | tf_op jit(solution)/shard_map/spread_left/pallas_call | solution.py:141
  40.8 2.7 %collective-permute-start = (bf16[512,256]{1,0:T(8,128)(2,1)}, bf16[512,256]{1,0:T(8,128)(2,1)S(1)}, u32[]{:S(2)}, u32[]{:S(2)}) collective-permute-start(bf16[512,256]{1,0:T(8,128)(2,1)} %spread_left.1.own_ref), channel_id=1, source_target_pairs={{0,1},{1,0},{2,3},{3,2},{4,5},{5,4},{6,7},{7,6},{8,9},{9,8},{10,11... | collective-permute-start | bytes 786440 | tf_op jit(solution)/shard_map/ppermute | solution.py:151
  43.5 2.4 %spread_right.1.right_ref = bf16[512,256]{1,0:T(8,128)(2,1)} custom-call(bf16[2048,128]{1,0:T(8,128)(2,1)} %bitcast.10), custom_call_target="tpu_custom_call" | custom-call | flops 4194304 | bytes 1048576 | tf_op jit(solution)/shard_map/spread_right/pallas_call | solution.py:141
  46.0 0.0 collective-permute-done.other_ref
  46.0 0.0 copy-start.1
  46.0 0.7 copy-done.1
  46.7 2.3 %mix.1 = bf16[1024,128]{1,0:T(8,128)(2,1)} custom-call(s32[1]{0:T(128)} %bitcast.core_ref, bf16[512,256]{1,0:T(8,128)(2,1)} %spread_left.1.own_ref, bf16[512,256]{1,0:T(8,128)(2,1)} %copy-done.1, bf16[512,256]{1,0:T(8,128)(2,1)} %spread_right.1.right_ref), custom_call_target="tpu_custom_call" | custom-call | tf_op jit(solution)/shard_map/mix/pallas_call | solution.py:153
  49.0 6.2 %all-to-all-start.1 = ((bf16[128,8,128]{2,1,0:T(8,128)(2,1)}), bf16[128,8,128]{2,1,0:T(8,128)(2,1)S(1)}, u32[]{:S(2)}, u32[]{:S(2)}) async-start(bf16[128,8,128]{2,1,0:T(8,128)(2,1)} %bitcast.12), calls=%async_computation.1 | async-start | bytes 524288 | tf_op jit(solution)/shard_map/all_to_all | solution.py:160
  55.2 2.0 %gate.1.gate_ref = f32[1024,128]{1,0:T(8,128)} custom-call(bf16[1024,128]{1,0:T(8,128)(2,1)} %get-tuple-element.8.normed_ref, bf16[128,640]{1,0:T(8,128)(2,1)} %w_ref.4), custom_call_target="tpu_custom_call" | custom-call | flops 33554432 | bytes 1048576 | tf_op jit(solution)/shard_map/gate/pallas_call | solution.py:131
  57.2 12.9 %all-to-all-done.1 = bf16[128,8,128]{2,1,0:T(8,128)(2,1)S(1)} async-done(((bf16[128,8,128]{2,1,0:T(8,128)(2,1)}), bf16[128,8,128]{2,1,0:T(8,128)(2,1)S(1)}, u32[]{:S(2)}, u32[]{:S(2)}) %all-to-all-start.1) | async-done | bytes 262176 | tf_op jit(solution)/shard_map/all_to_all | solution.py:160
  70.1 0.0 copy-start
  70.1 0.7 copy-done
  70.8 2.5 %output.1 = bf16[1024,128]{1,0:T(8,128)(2,1)} custom-call(bf16[1024,128]{1,0:T(8,128)(2,1)} %bitcast.11, f32[1024,128]{1,0:T(8,128)} %gate.1.gate_ref, f32[128]{0:T(128)} %gain_ref.1, f32[128]{0:T(128)} %shift_ref.1, bf16[128,128]{1,0:T(8,128)(2,1)} %w_ref.5), custom_call_target="tpu_custom_call" | custom-call | tf_op jit(solution)/shard_map/output/pallas_call | solution.py:161
Async XLA Ops:
  40.8 5.1 %collective-permute-start = (bf16[512,256]{1,0:T(8,128)(2,1)}, bf16[512,256]{1,0:T(8,128)(2,1)S(1)}, u32[]{:S(2)}, u32[]{:S(2)}) collective-permute-start(bf16[512,256]{1,0:T(8,128)(2,1)} %spread_left.1.own_ref), channel_id=1, source_target_pairs={{0,1},{1,0},{2,3},{3,2},{4,5},{5,4},{6,7},{7,6},{8,9},{9,8},{10,11... | collective-permute-start | bytes 786440 | tf_op jit(solution)/shard_map/ppermute | solution.py:151
  46.0 0.7 copy-start.1
  49.0 21.1 %all-to-all-start.1 = ((bf16[128,8,128]{2,1,0:T(8,128)(2,1)}), bf16[128,8,128]{2,1,0:T(8,128)(2,1)S(1)}, u32[]{:S(2)}, u32[]{:S(2)}) async-start(bf16[128,8,128]{2,1,0:T(8,128)(2,1)} %bitcast.12), calls=%async_computation.1 | async-start | bytes 524288 | tf_op jit(solution)/shard_map/all_to_all | solution.py:160
  70.1 0.7 copy-start

commit v2 on v1

--- a/solution.py
+++ b/solution.py
@@ -11,6 +11,7 @@
 BF16 = jnp.bfloat16
 VMEM = pl.BlockSpec(memory_space=pltpu.VMEM)
 SMEM = pl.BlockSpec(memory_space=pltpu.SMEM)
+SMALL = pltpu.CompilerParams(vmem_limit_bytes=12 << 20)
 
 
 def swap_groups(v):
@@ -55,33 +56,57 @@
     )
 
 
-def spread_kernel(offset, recv_ref, out_ref):
+def spread(recv_ref, offset):
+    out = []
     for r in range(16):
+        halves = []
         for g in range(2):
             base = (r * 8 + g * 4) * 16
             v = [
                 recv_ref[base + c * 16 : base + c * 16 + 16, :].astype(F32)[offset : offset + 8]
                 for c in range(4)
             ]
-            out_ref[r * 32 : (r + 1) * 32, g * 128 : (g + 1) * 128] = jnp.concatenate(
-                swap_groups(v), axis=0
-            ).astype(BF16)
-
-
-def mix_kernel(core_ref, own_ref, other_ref, right_ref, out_ref):
+            halves.append(jnp.concatenate(swap_groups(v), axis=0).astype(BF16))
+        out.append(halves)
+    return out
+
+
+def gather_pieces(mixed, q, g):
+    v = mixed[q * 32 : (q + 1) * 32, g * 128 : (g + 1) * 128]
+    v = [v[b * 8 : (b + 1) * 8] for b in range(4)]
+    return jnp.concatenate(swap_groups(v), axis=0).astype(BF16)
+
+
+def store_spread(recv_ref, offset, out_ref):
+    for r, halves in enumerate(spread(recv_ref, offset)):
+        for g in range(2):
+            out_ref[r * 32 : (r + 1) * 32, g * 128 : (g + 1) * 128] = halves[g]
+
+
+def own_kernel(recv_ref, right_ref, out_ref, left_ref):
+    store_spread(recv_ref, 0, left_ref)
+    store_spread(recv_ref, 8, right_ref)
+    mixed = lax.dot_general(
+        left_ref[...], right_ref[...], (((0,), (0,)), ((), ())), preferred_element_type=F32
+    )
+    for q in range(8):
+        for g in range(2):
+            out_ref[q * 64 + g * 32 : q * 64 + g * 32 + 32, :] = gather_pieces(mixed, q, g)
+
+
+def other_kernel(core_ref, recv_ref, right_ref, own_ref, out_ref, left_ref):
     core = core_ref[0]
-    right = right_ref[...]
-    for part, ref in ((core, own_ref), (1 - core, other_ref)):
-        mixed = lax.dot_general(
-            ref[...], right, (((0,), (0,)), ((), ())), preferred_element_type=F32
-        )
-        for q in range(8):
-            row = 2 * q + part
-            for g in range(2):
-                v = mixed[q * 32 : (q + 1) * 32, g * 128 : (g + 1) * 128]
-                v = [v[b * 8 : (b + 1) * 8] for b in range(4)]
-                start = pl.multiple_of(row * 64 + g * 32, 32)
-                out_ref[pl.ds(start, 32), :] = jnp.concatenate(swap_groups(v), axis=0).astype(BF16)
+    for q in range(8):
+        start = pl.multiple_of((2 * q + core) * 64, 64)
+        out_ref[pl.ds(start, 64), :] = own_ref[q * 64 : (q + 1) * 64, :]
+    store_spread(recv_ref, 0, left_ref)
+    mixed = lax.dot_general(
+        left_ref[...], right_ref[...], (((0,), (0,)), ((), ())), preferred_element_type=F32
+    )
+    for q in range(8):
+        for g in range(2):
+            start = pl.multiple_of((2 * q + 1 - core) * 64 + g * 32, 32)
+            out_ref[pl.ds(start, 32), :] = gather_pieces(mixed, q, g)
 
 
 def output_kernel(recv_ref, gate_ref, gain_ref, shift_ref, w_ref, out_ref, scr_ref):
@@ -125,6 +150,7 @@
         in_specs=[VMEM] * 4,
         out_specs=(VMEM, VMEM),
         scratch_shapes=[pltpu.VMEM((2048, 128), F32)],
+        compiler_params=SMALL,
         name="project",
     )(pair.reshape(1024, 128), norm_in.reshape(1, 128), shift_in.reshape(1, 128), in_weight)
     recv = lax.all_to_all(msg.reshape(128, 16, 128), CHIPS, 0, 0, tiled=True).reshape(2048, 128)
@@ -133,30 +159,34 @@
         out_shape=jax.ShapeDtypeStruct((1024, 128), F32),
         in_specs=[VMEM] * 2,
         out_specs=VMEM,
+        compiler_params=SMALL,
         name="gate",
         cost_estimate=pl.CostEstimate(flops=1 << 25, bytes_accessed=1 << 20, transcendentals=1 << 17),
     )(normed, in_weight)
 
-    def spread(offset, name):
-        return pl.pallas_call(
-            lambda a, b: spread_kernel(offset, a, b),
-            out_shape=jax.ShapeDtypeStruct((512, 256), BF16),
-            in_specs=[VMEM],
-            out_specs=VMEM,
-            name=name,
-            cost_estimate=pl.CostEstimate(flops=1 << 22, bytes_accessed=1 << 20, transcendentals=0),
-        )(recv)
-
-    own = spread(0, "spread_left")
-    other = lax.ppermute(own, "core", [(0, 1), (1, 0)])
-    right = spread(8, "spread_right")
+    other = lax.ppermute(recv, "core", [(0, 1), (1, 0)])
+    right, own = pl.pallas_call(
+        own_kernel,
+        out_shape=(
+            jax.ShapeDtypeStruct((512, 256), BF16),
+            jax.ShapeDtypeStruct((512, 128), BF16),
+        ),
+        in_specs=[VMEM],
+        out_specs=(VMEM, VMEM),
+        scratch_shapes=[pltpu.VMEM((512, 256), BF16)],
+        compiler_params=SMALL,
+        name="own",
+        cost_estimate=pl.CostEstimate(flops=1 << 26, bytes_accessed=1 << 20, transcendentals=0),
+    )(recv)
     back = pl.pallas_call(
-        mix_kernel,
+        other_kernel,
         out_shape=jax.ShapeDtypeStruct((1024, 128), BF16),
         in_specs=[SMEM, VMEM, VMEM, VMEM],
         out_specs=VMEM,
-        name="mix",
-    )(core, own, other, right)
+        scratch_shapes=[pltpu.VMEM((512, 256), BF16)],
+        compiler_params=SMALL,
+        name="other",
+    )(core, other, right, own)
     mixed = lax.all_to_all(back.reshape(128, 8, 128), CHIPS, 0, 0, tiled=True).reshape(1024, 128)
     out = pl.pallas_call(
         output_kernel,
@@ -164,6 +194,7 @@
         in_specs=[VMEM, VMEM, SMEM, SMEM, VMEM],
         out_specs=VMEM,
         scratch_shapes=[pltpu.VMEM((1024, 128), F32)],
+        compiler_params=SMALL,
         name="output",
     )(mixed, gate, norm_out, shift_out, out_weight)
     return out.reshape(pair.shape)

time: 73.6 us -> 69.2 us (0.940)
  Pallas kernels: 14.8 us -> 7.61 us
  waiting for transfers between devices: 12.9 us -> 14.6 us
  local copies, waits for them, and re-layouts: 1.39 us -> 2.56 us
    pallas_call x3 -> x2, Pallas kernels: 7.2 us -> 4.26 us  [the longest x1 2.86 us: local(): pl.pallas_call(own_kernel, out_shape=(jax.ShapeDtypeStruct((512, 256), BF...]
    pallas_call x1, Pallas kernels: 3.06 us -> 1.22 us  [local(): pl.pallas_call(project_kernel, out_shape=(jax.ShapeDtypeStruct((2048, 128...]
    pallas_call x1, Pallas kernels: 2.01 us -> 0.22 us  [local(): pl.pallas_call(gate_kernel, out_shape=jax.ShapeDtypeStruct((1024, 128), F...]
    all_to_all x1, waiting for transfers between devices: 12.9 us -> 14.6 us  [local(): lax.all_to_all(back.reshape(128, 8, 128), CHIPS, 0, 0, tiled=True)]
    unnamed x4 -> x16, local copies, waits for them, and re-layouts: 1.39 us -> 2.56 us
  transfers between devices with their start and end apart: 2 -> 2, of which waited for: 1 -> 1; matrix products, arithmetic and copies ran while one was open for 0% -> 0% of each run, Pallas kernels for 6% -> 4%
where the time goes in v2:
time: 69.2 us; the launch traced here: 68.9 us
  blocking collectives  35.1 us (51%)
  waiting for transfers between devices  14.6 us (21%)
  starting transfers between devices  9 us (13%)
  Pallas kernels  7.61 us (11%)
  local copies, waits for them, and re-layouts  2.56 us (4%)
    all_to_all x1, blocking collectives, local(): lax.all_to_all(msg.reshape(128, 16, 128), CHIPS, 0, 0, tiled=True)  35.1 us
    all_to_all x1, waiting for transfers between devices, local(): lax.all_to_all(back.reshape(128, 8, 128), CHIPS, 0, 0, tiled=True)  14.6 us
    all_to_all x1, starting transfers between devices, local(): lax.all_to_all(back.reshape(128, 8, 128), CHIPS, 0, 0, tiled=True)  6.31 us
    pallas_call x1, Pallas kernels, local(): pl.pallas_call(own_kernel, out_shape=(jax.ShapeDtypeStruct((512, 256), BF...  2.86 us
    ppermute x1, starting transfers between devices, local(): other = lax.ppermute(recv, 'core', [(0, 1), (1, 0)])  2.69 us
    unnamed x16, local copies, waits for them, and re-layouts  2.56 us
    pallas_call x1, Pallas kernels, local(): pl.pallas_call(output_kernel, out_shape=jax.ShapeDtypeStruct((1024, 128),...  1.91 us
    pallas_call x1, Pallas kernels, local(): pl.pallas_call(other_kernel, out_shape=jax.ShapeDtypeStruct((1024, 128),...  1.4 us
  transfers between devices with their start and end apart: 2, of which 1 were waited for; matrix products, arithmetic and copies ran while one was open for 0% of the time, Pallas kernels for 4%

profile of v2, /device:TPU:1, one launch (start us, length us, event | category | flops | bytes accessed | tf_op | source)
XLA Modules:
  0.0 68.9 jit_solution(14319634802952387622)
XLA Ops:
  0.0 0.0 copy-start.6
  0.0 0.0 copy-start.7
  0.0 0.7 copy-done.6
  0.7 0.0 copy-done.7
  0.7 0.0 copy-start
  0.7 0.9 %copy-done = bf16[128,640]{1,0:T(8,128)(2,1)S(1)} copy-done((bf16[128,640]{1,0:T(8,128)(2,1)S(1)}, bf16[128,640]{1,0:T(8,128)(2,1)}, u32[]{:S(2)}) %copy-start) | copy-done | bytes 163864
  1.6 0.0 copy-start.2
  1.6 0.9 %copy-done.2 = bf16[32,32,128]{2,1,0:T(8,128)(2,1)S(1)} copy-done((bf16[32,32,128]{2,1,0:T(8,128)(2,1)S(1)}, bf16[32,32,128]{2,1,0:T(8,128)(2,1)}, u32[]{:S(2)}) %copy-start.2) | copy-done | bytes 262168
  2.5 1.2 %project.1 = (bf16[2048,128]{1,0:T(8,128)(2,1)S(1)}, bf16[1024,128]{1,0:T(8,128)(2,1)S(1)}) custom-call(bf16[1024,128]{1,0:T(8,128)(2,1)S(1)} %bitcast.13, f32[1,128]{1,0:T(1,128)S(1)} %bitcast.14, f32[1,128]{1,0:T(1,128)S(1)} %bitcast.15, bf16[128,640]{1,0:T(8,128)(2,1)S(1)} %copy-done), custom_call_target="tpu_custom_call" | custom-call | tf_op jit(solution)/shard_map/project/pallas_call | solution.py:144
  3.8 35.1 %all_to_all.10 = bf16[128,16,128]{2,1,0:T(8,128)(2,1)S(1)} all-to-all(bf16[128,16,128]{2,1,0:T(8,128)(2,1)S(1)} %bitcast.12), channel_id=1, replica_groups=mesh['xh'=2,'z'=8,'xl'=2,'y'=4,'core'=2] {'xh','z','xl','y'}, dimensions={0} | all-to-all | bytes 1048576 | tf_op jit(solution)/shard_map/all_to_all | solution.py:156
  38.9 2.7 %collective-permute-start = (bf16[2048,128]{1,0:T(8,128)(2,1)S(1)}, bf16[2048,128]{1,0:T(8,128)(2,1)S(1)}, u32[]{:S(2)}, u32[]{:S(2)}) collective-permute-start(bf16[2048,128]{1,0:T(8,128)(2,1)S(1)} %bitcast.9), channel_id=1, source_target_pairs={{0,1},{1,0},{2,3},{3,2},{4,5},{5,4},{6,7},{7,6},{8,9},{9,8},{10,11... | collective-permute-start | bytes 1572872 | tf_op jit(solution)/shard_map/ppermute | solution.py:167
  41.6 2.9 %own.1 = (bf16[512,256]{1,0:T(8,128)(2,1)S(1)}, bf16[512,128]{1,0:T(8,128)(2,1)S(1)}) custom-call(bf16[2048,128]{1,0:T(8,128)(2,1)S(1)} %bitcast.10), custom_call_target="tpu_custom_call" | custom-call | flops 67108864 | bytes 1048576 | tf_op jit(solution)/shard_map/own/pallas_call | solution.py:168
  44.4 0.0 collective-permute-done.recv_ref
  44.4 1.4 %other.1 = bf16[1024,128]{1,0:T(8,128)(2,1)} custom-call(s32[1]{0:T(128)} %bitcast.core_ref, bf16[2048,128]{1,0:T(8,128)(2,1)S(1)} %collective-permute-done.recv_ref, bf16[512,256]{1,0:T(8,128)(2,1)S(1)} %get-tuple-element.10.right_ref, bf16[512,128]{1,0:T(8,128)(2,1)S(1)} %get-tuple-element.11.own_ref), custom_call_target="tpu_custom_call" | custom-call | tf_op jit(solution)/shard_map/other/pallas_call | solution.py:181
  45.8 0.0 copy-start.1
  45.8 6.3 %all-to-all-start.1 = ((bf16[128,8,128]{2,1,0:T(8,128)(2,1)}), bf16[128,8,128]{2,1,0:T(8,128)(2,1)S(1)}, u32[]{:S(2)}, u32[]{:S(2)}) async-start(bf16[128,8,128]{2,1,0:T(8,128)(2,1)} %bitcast.6), calls=%async_computation.1 | async-start | bytes 524288 | tf_op jit(solution)/shard_map/all_to_all | solution.py:190
  52.1 0.0 copy-done.1
  52.1 0.0 copy-start.3
  52.2 0.2 gate.1.gate_ref
  52.4 0.0 copy-start.4
  52.4 0.0 copy-start.5
  52.4 14.6 %all-to-all-done.1 = bf16[128,8,128]{2,1,0:T(8,128)(2,1)S(1)} async-done(((bf16[128,8,128]{2,1,0:T(8,128)(2,1)}), bf16[128,8,128]{2,1,0:T(8,128)(2,1)S(1)}, u32[]{:S(2)}, u32[]{:S(2)}) %all-to-all-start.1) | async-done | bytes 262176 | tf_op jit(solution)/shard_map/all_to_all | solution.py:190
  67.0 0.0 copy-done.3
  67.0 0.0 copy-done.4
  67.0 0.0 copy-done.5
  67.0 1.9 %output.1 = bf16[1024,128]{1,0:T(8,128)(2,1)} custom-call(bf16[1024,128]{1,0:T(8,128)(2,1)S(1)} %bitcast.11, f32[1024,128]{1,0:T(8,128)S(1)} %gate.1.gate_ref, f32[128]{0:T(128)S(1)} %copy-done.4, f32[128]{0:T(128)S(1)} %copy-done.5, bf16[128,128]{1,0:T(8,128)(2,1)S(1)} %copy-done.3), custom_call_target="tpu_custom_call" | custom-call | tf_op jit(solution)/shard_map/output/pallas_call | solution.py:191
Async XLA Ops:
  0.0 0.7 copy-start.6
  0.0 0.7 copy-start.7
  0.7 0.9 %copy-start = (bf16[128,640]{1,0:T(8,128)(2,1)S(1)}, bf16[128,640]{1,0:T(8,128)(2,1)}, u32[]{:S(2)}) copy-start(bf16[128,640]{1,0:T(8,128)(2,1)} %w_ref.4) | copy-start | bytes 491524
  1.6 0.9 %copy-start.2 = (bf16[32,32,128]{2,1,0:T(8,128)(2,1)S(1)}, bf16[32,32,128]{2,1,0:T(8,128)(2,1)}, u32[]{:S(2)}) copy-start(bf16[32,32,128]{2,1,0:T(8,128)(2,1)} %param.7) | copy-start | bytes 786436
  38.9 5.6 %collective-permute-start = (bf16[2048,128]{1,0:T(8,128)(2,1)S(1)}, bf16[2048,128]{1,0:T(8,128)(2,1)S(1)}, u32[]{:S(2)}, u32[]{:S(2)}) collective-permute-start(bf16[2048,128]{1,0:T(8,128)(2,1)S(1)} %bitcast.9), channel_id=1, source_target_pairs={{0,1},{1,0},{2,3},{3,2},{4,5},{5,4},{6,7},{7,6},{8,9},{9,8},{10,11... | collective-permute-start | bytes 1572872 | tf_op jit(solution)/shard_map/ppermute | solution.py:167
  45.8 6.3 %copy-start.1 = (bf16[128,640]{1,0:T(8,128)(2,1)S(1)}, bf16[128,640]{1,0:T(8,128)(2,1)}, u32[]{:S(2)}) copy-start(bf16[128,640]{1,0:T(8,128)(2,1)} %w_ref.4) | copy-start | bytes 491524
  45.8 21.2 %all-to-all-start.1 = ((bf16[128,8,128]{2,1,0:T(8,128)(2,1)}), bf16[128,8,128]{2,1,0:T(8,128)(2,1)S(1)}, u32[]{:S(2)}, u32[]{:S(2)}) async-start(bf16[128,8,128]{2,1,0:T(8,128)(2,1)} %bitcast.6), calls=%async_computation.1 | async-start | bytes 524288 | tf_op jit(solution)/shard_map/all_to_all | solution.py:190
  52.1 14.9 %copy-start.3 = (bf16[128,128]{1,0:T(8,128)(2,1)S(1)}, bf16[128,128]{1,0:T(8,128)(2,1)}, u32[]{:S(2)}) copy-start(bf16[128,128]{1,0:T(8,128)(2,1)} %w_ref.5) | copy-start | bytes 98308
  52.4 14.6 %copy-start.4 = (f32[128]{0:T(128)S(1)}, f32[128]{0:T(128)}, u32[]{:S(2)}) copy-start(f32[128]{0:T(128)} %gain_ref.1) | copy-start | bytes 1540
  52.4 14.6 %copy-start.5 = (f32[128]{0:T(128)S(1)}, f32[128]{0:T(128)}, u32[]{:S(2)}) copy-start(f32[128]{0:T(128)} %shift_ref.1) | copy-start | bytes 1540

commit v3 on v2

v3 whole, which is shorter than its diff:
```python
import functools

import jax
import jax.numpy as jnp
from jax import lax
from jax.experimental import pallas as pl
from jax.experimental.pallas import tpu as pltpu
from jax.sharding import Mesh, PartitionSpec as P

EPSILON = 1e-05
CHIPS = ("xh", "z", "xl", "y")
F32 = jnp.float32
BF16 = jnp.bfloat16
VMEM = pl.BlockSpec(memory_space=pltpu.VMEM)
SMEM = pl.BlockSpec(memory_space=pltpu.SMEM)
HBM = pl.BlockSpec(memory_space=pltpu.HBM)
UNROLL = 8
SMALL = pltpu.CompilerParams(vmem_limit_bytes=12 << 20)


def swap_groups(v):
    lane = lax.broadcasted_iota(jnp.int32, v[0].shape, 1)
    low = lane < 64
    u = [None] * 4
    for c in (0, 1):
        a, b = v[c], v[c + 2]
        u[c] = jnp.where(low, a, pltpu.roll(b, 64, 1))
        u[c + 2] = jnp.where(low, pltpu.roll(a, 64, 1), b)
    even = (lane & 32) == 0
    out = [None] * 4
    for c in (0, 2):
        a, b = u[c], u[c + 1]
        out[c] = jnp.where(even, a, pltpu.roll(b, 32, 1))
        out[c + 1] = jnp.where(even, pltpu.roll(a, 96, 1), b)
    return out


def project_kernel(
    pair_hbm,
    gain_hbm,
    shift_hbm,
    w_hbm,
    gain_out_hbm,
    shift_out_hbm,
    w_out_hbm,
    msg_ref,
    gate_ref,
    gain_col_ref,
    shift_col_ref,
    w_out_ref,
    pair_ref,
    w_ref,
    rows_ref,
    scr_ref,
    sem,
):
    def pair_copy(t):
        rows = slice(t * 256, (t + 1) * 256)
        return pltpu.make_async_copy(pair_hbm.at[rows], pair_ref.at[rows], sem.at[6 + t])

    w_copy = pltpu.make_async_copy(w_hbm, w_ref, sem.at[0])
    small = [
        pltpu.make_async_copy(ref, rows_ref.at[pl.ds(t * 8, 1)], sem.at[1 + t])
        for t, ref in enumerate((gain_hbm, shift_hbm, gain_out_hbm, shift_out_hbm))
    ]
    w_out_copy = pltpu.make_async_copy(w_out_hbm, w_out_ref, sem.at[5])
    w_copy.start()
    small[0].start()
    small[1].start()
    for t in range(4):
        pair_copy(t).start()
    small[2].start()
    small[3].start()
    w_out_copy.start()
    w_copy.wait()
    wt = jnp.transpose(w_ref[:, :512].astype(F32)).astype(BF16)
    wg = w_ref[:, 512:640]
    small[0].wait()
    small[1].wait()
    gain = rows_ref[0:1, :]
    shift = rows_ref[8:9, :]
    for a in range(8):
        if a % 2 == 0:
            pair_copy(a // 2).wait()
        x = pair_ref[a * 128 : (a + 1) * 128, :].astype(F32)
        center = jnp.mean(x, axis=-1, keepdims=True)
        d = x - center
        spread = jnp.mean(d * d, axis=-1, keepdims=True)
        n = (d * lax.rsqrt(spread + EPSILON) * gain + shift).astype(BF16)
        p = lax.dot_general(wt, n, (((1,), (1,)), ((), ())), preferred_element_type=F32)
        left = jax.nn.sigmoid(p[0:128]) * p[128:256]
        right = jax.nn.sigmoid(p[256:384]) * p[384:512]
        scr_ref[pl.ds(a, 128, stride=16), :] = left
        scr_ref[pl.ds(8 + a, 128, stride=16), :] = right
        gate_ref[a * 128 : (a + 1) * 128, :] = jax.nn.sigmoid(
            jnp.dot(n, wg, preferred_element_type=F32)
        )
    msg_ref[...] = scr_ref[...].astype(BF16)
    small[2].wait()
    small[3].wait()
    gain_col_ref[...] = jnp.transpose(jnp.broadcast_to(rows_ref[16:17, :], (128, 128)))
    shift_col_ref[...] = jnp.transpose(jnp.broadcast_to(rows_ref[24:25, :], (128, 128)))
    w_out_copy.wait()


def spread_kernel(offset, recv_ref, out_ref):
    def step(t, carry):
        for u in range(UNROLL):
            r = t * UNROLL + u
            for g in range(2):
                base = r * 128 + g * 64
                v = []
                for c in range(4):
                    start = pl.multiple_of(base + c * 16, 16)
                    piece = recv_ref[pl.ds(start, 16), :].astype(F32)
                    v.append(piece[offset : offset + 8])
                out_ref[pl.ds(pl.multiple_of(r * 32, 32), 32), g * 128 : (g + 1) * 128] = (
                    jnp.concatenate(swap_groups(v), axis=0).astype(BF16)
                )
        return carry

    lax.fori_loop(0, 16 // UNROLL, step, 0)


def multiply(left_ref, right_ref, mixed_ref):
    mixed_ref[...] = lax.dot_general(
        left_ref[...], right_ref[...], (((0,), (0,)), ((), ())), preferred_element_type=F32
    )


def pieces(mixed_ref, out_ref, row_of):
    def step(t, carry):
        for u in range(4):
            q = t * 4 + u
            for g in range(2):
                v = []
                for b in range(4):
                    start = pl.multiple_of(q * 32 + b * 8, 8)
                    v.append(mixed_ref[pl.ds(start, 8), g * 128 : (g + 1) * 128])
                start = pl.multiple_of(row_of(q) * 64 + g * 32, 32)
                out_ref[pl.ds(start, 32), :] = jnp.concatenate(swap_groups(v), axis=0).astype(BF16)
        return carry

    lax.fori_loop(0, 2, step, 0)


def own_kernel(recv_ref, left_ref, right_ref, out_ref, mixed_ref):
    spread_kernel(8, recv_ref, right_ref)
    multiply(left_ref, right_ref, mixed_ref)
    pieces(mixed_ref, out_ref, lambda q: q)


def other_kernel(core_ref, left_ref, right_ref, own_ref, out_ref, mixed_ref):
    core = core_ref[0]
    multiply(left_ref, right_ref, mixed_ref)
    for q in range(8):
        start = pl.multiple_of((2 * q + core) * 64, 64)
        out_ref[pl.ds(start, 64), :] = own_ref[q * 64 : (q + 1) * 64, :]
    pieces(mixed_ref, out_ref, lambda q: 2 * q + 1 - core)


def output_kernel(recv_ref, gate_ref, gain_ref, shift_ref, w_ref, out_ref, scr_ref):
    def total_step(t, sums):
        sums = list(sums)
        for u in range(16):
            rows = pl.ds(pl.multiple_of(t * 256 + u * 16, 16), 16)
            x = recv_ref[rows, :].astype(F32)
            scr_ref[rows, :] = x
            sums[u % 4] = sums[u % 4] + (x[0:8] + x[8:16])
        return tuple(sums)

    zero = jnp.zeros((8, 128), F32)
    sums = lax.fori_loop(0, 4, total_step, (zero,) * 4)
    center = ((sums[0] + sums[1]) + (sums[2] + sums[3])) * (1.0 / 128.0)

    def square_step(t, sums):
        sums = list(sums)
        for u in range(32):
            d = scr_ref[pl.ds(pl.multiple_of(t * 256 + u * 8, 8), 8), :] - center
            sums[u % 4] = sums[u % 4] + d * d
        return tuple(sums)

    sums = lax.fori_loop(0, 4, square_step, (zero,) * 4)
    spread = ((sums[0] + sums[1]) + (sums[2] + sums[3])) * (1.0 / 128.0)
    scale = lax.rsqrt(spread + EPSILON)
    w = w_ref[...]
    for s in range(8):
        x = scr_ref[pl.ds(s, 128, stride=8), :]
        x = (x - center[s : s + 1]) * scale[s : s + 1] * gain_ref[...] + shift_ref[...]
        o = lax.dot_general(
            x.astype(BF16), w, (((0,), (0,)), ((), ())), preferred_element_type=F32
        )
        for b in range(4):
            i = b * 8 + s
            rows = slice(i * 32, (i + 1) * 32)
            out_ref[rows, :] = (gate_ref[rows, :] * o[b * 32 : (b + 1) * 32]).astype(BF16)


def local(pair, norm_in, shift_in, in_weight, norm_out, shift_out, out_weight):
    core = lax.axis_index("core").astype(jnp.int32).reshape(1)
    shape = jax.ShapeDtypeStruct
    msg, gate, gain_col, shift_col, w_out = pl.pallas_call(
        project_kernel,
        out_shape=(
            shape((2048, 128), BF16),
            shape((1024, 128), F32),
            shape((128, 128), F32),
            shape((128, 128), F32),
            shape((128, 128), BF16),
        ),
        in_specs=[HBM] * 7,
        out_specs=(VMEM,) * 5,
        scratch_shapes=[
            pltpu.VMEM((1024, 128), BF16),
            pltpu.VMEM((128, 640), BF16),
            pltpu.VMEM((32, 128), F32),
            pltpu.VMEM((2048, 128), F32),
            pltpu.SemaphoreType.DMA((10,)),
        ],
        compiler_params=SMALL,
        name="project",
    )(
        pair.reshape(1024, 128),
        norm_in.reshape(1, 128),
        shift_in.reshape(1, 128),
        in_weight,
        norm_out.reshape(1, 128),
        shift_out.reshape(1, 128),
        out_weight,
    )
    recv = lax.all_to_all(msg.reshape(128, 16, 128), CHIPS, 0, 0, tiled=True).reshape(2048, 128)
    left = pl.pallas_call(
        functools.partial(spread_kernel, 0),
        out_shape=shape((512, 256), BF16),
        in_specs=[VMEM],
        out_specs=VMEM,
        compiler_params=SMALL,
        name="spread",
    )(recv)
    other = lax.ppermute(left, "core", [(0, 1), (1, 0)])
    right, own = pl.pallas_call(
        own_kernel,
        out_shape=(shape((512, 256), BF16), shape((512, 128), BF16)),
        in_specs=[VMEM, VMEM],
        out_specs=(VMEM, VMEM),
        scratch_shapes=[pltpu.VMEM((256, 256), F32)],
        compiler_params=SMALL,
        name="own",
        cost_estimate=pl.CostEstimate(flops=1 << 26, bytes_accessed=1 << 20, transcendentals=0),
    )(recv, left)
    back = pl.pallas_call(
        other_kernel,
        out_shape=shape((1024, 128), BF16),
        in_specs=[SMEM, VMEM, VMEM, VMEM],
        out_specs=VMEM,
        scratch_shapes=[pltpu.VMEM((256, 256), F32)],
        compiler_params=SMALL,
        name="other",
    )(core, other, right, own)
    mixed = lax.all_to_all(back.reshape(128, 8, 128), CHIPS, 0, 0, tiled=True).reshape(1024, 128)
    out = pl.pallas_call(
        output_kernel,
        out_shape=shape((1024, 128), BF16),
        in_specs=[VMEM] * 5,
        out_specs=VMEM,
        scratch_shapes=[pltpu.VMEM((1024, 128), F32)],
        compiler_params=SMALL,
        name="output",
    )(mixed, gate, gain_col, shift_col, w_out)
    return out.reshape(pair.shape)


def solution(mesh):
    fine = Mesh(mesh.devices.reshape(2, 8, 2, 4, 2), ("xh", "z", "xl", "y", "core"))
    spec = P(("xh", "z"), ("xl", "y", "core"), None)
    in_specs = (spec, P(), P(), P(), P(), P(), P())
    return jax.shard_map(local, mesh=fine, in_specs=in_specs, out_specs=spec, check_vma=False)
```

time: 69.2 us -> 67.3 us (0.973)
  blocking collectives: 35.1 us -> 54.6 us
  waiting for transfers between devices: 14.6 us -> 0.16 us
  starting transfers between devices: 9 us -> 2.78 us
  Pallas kernels: 7.61 us -> 6.08 us
  local copies, waits for them, and re-layouts: 2.56 us -> 3.31 us
    all_to_all x0 -> x1, blocking collectives: none -> 19.5 us  [local(): lax.all_to_all(back.reshape(128, 8, 128), CHIPS, 0, 0, tiled=True)]
    all_to_all x1 -> x0, waiting for transfers between devices: 14.6 us -> none  [local(): lax.all_to_all(back.reshape(128, 8, 128), CHIPS, 0, 0, tiled=True)]
    all_to_all x1 -> x0, starting transfers between devices: 6.31 us -> none  [local(): lax.all_to_all(back.reshape(128, 8, 128), CHIPS, 0, 0, tiled=True)]
    pallas_call x5, Pallas kernels: 7.61 us -> 6.08 us  [the longest x1 2.93 us: local(): pl.pallas_call(project_kernel, out_shape=(shape((2048, 128), BF16), shape...]
    unnamed x16 -> x14, local copies, waits for them, and re-layouts: 2.56 us -> 3.31 us
  transfers between devices with their start and end apart: 2 -> 1, of which waited for: 1 -> 1; matrix products, arithmetic and copies ran while one was open for 0% -> 0% of each run, Pallas kernels for 4% -> 1%
where the time goes in v3:
time: 67.3 us; the launch traced here: 67 us
  blocking collectives  54.6 us (81%)
  Pallas kernels  6.08 us (9%)
  local copies, waits for them, and re-layouts  3.31 us (5%)
  starting transfers between devices  2.78 us (4%)
    all_to_all x1, blocking collectives, local(): lax.all_to_all(msg.reshape(128, 16, 128), CHIPS, 0, 0, tiled=True)  35.1 us
    all_to_all x1, blocking collectives, local(): lax.all_to_all(back.reshape(128, 8, 128), CHIPS, 0, 0, tiled=True)  19.5 us
    unnamed x14, local copies, waits for them, and re-layouts  3.31 us
    pallas_call x1, Pallas kernels, local(): pl.pallas_call(project_kernel, out_shape=(shape((2048, 128), BF16), shape...  2.93 us
    ppermute x1, starting transfers between devices, local(): other = lax.ppermute(left, 'core', [(0, 1), (1, 0)])  2.78 us
  transfers between devices with their start and end apart: 1, of which 1 were waited for; matrix products, arithmetic and copies ran while one was open for 0% of the time, Pallas kernels for 1%

profile of v3, /device:TPU:1, one launch (start us, length us, event | category | flops | bytes accessed | tf_op | source)
XLA Modules:
  0.0 67.0 jit_solution(13950763287337944303)
XLA Ops:
  0.0 0.0 copy-start.6
  0.0 0.0 copy-start.3
  0.0 0.0 copy-start.4
  0.0 0.0 copy-start.5
  0.0 0.6 copy-done.6
  0.7 0.0 copy-done.3
  0.7 0.0 copy-done.4
  0.7 0.0 copy-done.5
  0.7 0.0 copy-start
  0.7 0.9 %copy-done = bf16[32,32,128]{2,1,0:T(8,128)(2,1)S(1)} copy-done((bf16[32,32,128]{2,1,0:T(8,128)(2,1)S(1)}, bf16[32,32,128]{2,1,0:T(8,128)(2,1)}, u32[]{:S(2)}) %copy-start) | copy-done | bytes 262168
  1.7 0.0 copy-start.1
  1.7 0.9 %copy-done.1 = bf16[128,640]{1,0:T(8,128)(2,1)S(1)} copy-done((bf16[128,640]{1,0:T(8,128)(2,1)S(1)}, bf16[128,640]{1,0:T(8,128)(2,1)}, u32[]{:S(2)}) %copy-start.1) | copy-done | bytes 163864
  2.6 0.0 copy-start.2
  2.6 0.8 %copy-done.2 = bf16[128,128]{1,0:T(8,128)(2,1)S(1)} copy-done((bf16[128,128]{1,0:T(8,128)(2,1)S(1)}, bf16[128,128]{1,0:T(8,128)(2,1)}, u32[]{:S(2)}) %copy-start.2) | copy-done | bytes 32792
  3.3 2.9 %project.1 = (bf16[2048,128]{1,0:T(8,128)(2,1)S(1)}, f32[1024,128]{1,0:T(8,128)S(1)}, f32[128,128]{1,0:T(8,128)S(1)}, f32[128,128]{1,0:T(8,128)S(1)}, bf16[128,128]{1,0:T(8,128)(2,1)S(1)}) custom-call(bf16[1024,128]{1,0:T(8,128)(2,1)S(1)} %bitcast.16, f32[1,128]{1,0:T(1,128)S(1)} %bitcast.17, f32[1,128]{1,0:T(1,128)S(1)} %bitcast.18, ...), custom_call_target="tpu_custom_call" | custom-call | tf_op jit(solution)/shard_map/project/pallas_call | solution.py:202
  6.3 35.1 %all_to_all.10 = bf16[128,16,128]{2,1,0:T(8,128)(2,1)S(1)} all-to-all(bf16[128,16,128]{2,1,0:T(8,128)(2,1)S(1)} %bitcast.15), channel_id=1, replica_groups=mesh['xh'=2,'z'=8,'xl'=2,'y'=4,'core'=2] {'xh','z','xl','y'}, dimensions={0} | all-to-all | bytes 1048576 | tf_op jit(solution)/shard_map/all_to_all | solution.py:231
  41.3 0.4 spread.1.left_ref
  41.8 2.8 %collective-permute-start = (bf16[512,256]{1,0:T(8,128)(2,1)S(1)}, bf16[512,256]{1,0:T(8,128)(2,1)S(1)}, u32[]{:S(2)}, u32[]{:S(2)}) collective-permute-start(bf16[512,256]{1,0:T(8,128)(2,1)S(1)} %spread.1.left_ref), channel_id=1, source_target_pairs={{0,1},{1,0},{2,3},{3,2},{4,5},{5,4},{6,7},{7,6},{8,9},{9,8},{10,11... | collective-permute-start | bytes 786440 | tf_op jit(solution)/shard_map/ppermute | solution.py:240
  44.5 1.0 %own.1 = (bf16[512,256]{1,0:T(8,128)(2,1)S(1)}, bf16[512,128]{1,0:T(8,128)(2,1)S(1)}) custom-call(bf16[2048,128]{1,0:T(8,128)(2,1)S(1)} %bitcast.12, bf16[512,256]{1,0:T(8,128)(2,1)S(1)} %spread.1.left_ref), custom_call_target="tpu_custom_call" | custom-call | flops 67108864 | bytes 1048576 | tf_op jit(solution)/shard_map/own/pallas_call | solution.py:241
  45.5 0.2 collective-permute-done.left_ref
  45.7 0.6 other.1
  46.3 19.5 %all_to_all.11 = bf16[128,8,128]{2,1,0:T(8,128)(2,1)S(1)} all-to-all(bf16[128,8,128]{2,1,0:T(8,128)(2,1)S(1)} %bitcast.14), channel_id=1, replica_groups=mesh['xh'=2,'z'=8,'xl'=2,'y'=4,'core'=2] {'xh','z','xl','y'}, dimensions={0} | all-to-all | bytes 524288 | tf_op jit(solution)/shard_map/all_to_all | solution.py:260
  65.9 1.1 %output.1 = bf16[1024,128]{1,0:T(8,128)(2,1)} custom-call(bf16[1024,128]{1,0:T(8,128)(2,1)S(1)} %bitcast.13, f32[1024,128]{1,0:T(8,128)S(1)} %get-tuple-element.15.gate_ref, f32[128,128]{1,0:T(8,128)S(1)} %get-tuple-element.16.gain_ref, f32[128,128]{1,0:T(8,128)S(1)} %get-tuple-element.17.shift_ref, bf16[128,128]{1,0:T(8,128)(2,1)S(1)} %get-tuple-element.18.w_ref), custom_call_target="tpu_custom_call" | custom-call | tf_op jit(solution)/shard_map/output/pallas_call | solution.py:261
Async XLA Ops:
  0.0 0.7 copy-start.6
  0.0 0.7 copy-start.3
  0.0 0.7 %copy-start.4 = (f32[128]{0:T(128)S(1)}, f32[128]{0:T(128)}, u32[]{:S(2)}) copy-start(f32[128]{0:T(128)} %param.9) | copy-start | bytes 1540
  0.0 0.7 %copy-start.5 = (f32[128]{0:T(128)S(1)}, f32[128]{0:T(128)}, u32[]{:S(2)}) copy-start(f32[128]{0:T(128)} %param.11) | copy-start | bytes 1540
  0.7 0.9 %copy-start = (bf16[32,32,128]{2,1,0:T(8,128)(2,1)S(1)}, bf16[32,32,128]{2,1,0:T(8,128)(2,1)}, u32[]{:S(2)}) copy-start(bf16[32,32,128]{2,1,0:T(8,128)(2,1)} %param.7) | copy-start | bytes 786436
  1.7 0.9 %copy-start.1 = (bf16[128,640]{1,0:T(8,128)(2,1)S(1)}, bf16[128,640]{1,0:T(8,128)(2,1)}, u32[]{:S(2)}) copy-start(bf16[128,640]{1,0:T(8,128)(2,1)} %w_hbm.1) | copy-start | bytes 491524
  2.6 0.8 %copy-start.2 = (bf16[128,128]{1,0:T(8,128)(2,1)S(1)}, bf16[128,128]{1,0:T(8,128)(2,1)}, u32[]{:S(2)}) copy-start(bf16[128,128]{1,0:T(8,128)(2,1)} %w_out_hbm.1) | copy-start | bytes 98308
  41.8 3.9 %collective-permute-start = (bf16[512,256]{1,0:T(8,128)(2,1)S(1)}, bf16[512,256]{1,0:T(8,128)(2,1)S(1)}, u32[]{:S(2)}, u32[]{:S(2)}) collective-permute-start(bf16[512,256]{1,0:T(8,128)(2,1)S(1)} %spread.1.left_ref), channel_id=1, source_target_pairs={{0,1},{1,0},{2,3},{3,2},{4,5},{5,4},{6,7},{7,6},{8,9},{9,8},{10,11... | collective-permute-start | bytes 786440 | tf_op jit(solution)/shard_map/ppermute | solution.py:240

commit v4 on v3

--- a/solution.py
+++ b/solution.py
@@ -1,4 +1,5 @@
 import functools
+import itertools
 
 import jax
 import jax.numpy as jnp
@@ -8,7 +9,9 @@
 from jax.sharding import Mesh, PartitionSpec as P
 
 EPSILON = 1e-05
-CHIPS = ("xh", "z", "xl", "y")
+AXES = ("xh", "z", "xl", "y", "core")
+ROOT = (1, 4, 0, 2)
+FLIP = (8 * ROOT[0] + ROOT[1]) ^ (8 * ROOT[2] + 2 * ROOT[3])
 F32 = jnp.float32
 BF16 = jnp.bfloat16
 VMEM = pl.BlockSpec(memory_space=pltpu.VMEM)
@@ -36,71 +39,93 @@
 
 
 def project_kernel(
-    pair_hbm,
-    gain_hbm,
-    shift_hbm,
-    w_hbm,
-    gain_out_hbm,
-    shift_out_hbm,
-    w_out_hbm,
-    msg_ref,
-    gate_ref,
-    gain_col_ref,
-    shift_col_ref,
-    w_out_ref,
-    pair_ref,
-    w_ref,
-    rows_ref,
-    scr_ref,
-    sem,
+    pair_hbm, gain_hbm, shift_hbm, w_hbm, gain_out_hbm, shift_out_hbm, msg_hbm, gate_hbm,
+    pair_ref, w_ref, rows_ref, normed_ref, scr_ref, msg_ref, gate_ref, sem, out_sem,
 ):
     def pair_copy(t):
-        rows = slice(t * 256, (t + 1) * 256)
-        return pltpu.make_async_copy(pair_hbm.at[rows], pair_ref.at[rows], sem.at[6 + t])
-
-    w_copy = pltpu.make_async_copy(w_hbm, w_ref, sem.at[0])
+        rows = pl.ds(t * 512, 512)
+        return pltpu.make_async_copy(pair_hbm.at[rows], pair_ref.at[rows], sem.at[5 + t])
+
+    def gate_copy(t, size):
+        rows = pl.ds(t * 512, size)
+        return pltpu.make_async_copy(gate_ref.at[rows], gate_hbm.at[rows], out_sem.at[4 + t])
+
+    def msg_copy(t):
+        rows = pl.ds(t * 512, 512)
+        return pltpu.make_async_copy(msg_ref.at[rows], msg_hbm.at[rows], out_sem.at[t])
+
     small = [
-        pltpu.make_async_copy(ref, rows_ref.at[pl.ds(t * 8, 1)], sem.at[1 + t])
+        pltpu.make_async_copy(ref, rows_ref.at[pl.ds(t * 8, 1)], sem.at[t])
         for t, ref in enumerate((gain_hbm, shift_hbm, gain_out_hbm, shift_out_hbm))
     ]
-    w_out_copy = pltpu.make_async_copy(w_out_hbm, w_out_ref, sem.at[5])
-    w_copy.start()
+    w_copy = pltpu.make_async_copy(w_hbm, w_ref, sem.at[4])
     small[0].start()
     small[1].start()
-    for t in range(4):
-        pair_copy(t).start()
+    pair_copy(0).start()
+    pair_copy(1).start()
+    w_copy.start()
     small[2].start()
     small[3].start()
-    w_out_copy.start()
-    w_copy.wait()
-    wt = jnp.transpose(w_ref[:, :512].astype(F32)).astype(BF16)
-    wg = w_ref[:, 512:640]
     small[0].wait()
     small[1].wait()
     gain = rows_ref[0:1, :]
     shift = rows_ref[8:9, :]
-    for a in range(8):
-        if a % 2 == 0:
-            pair_copy(a // 2).wait()
-        x = pair_ref[a * 128 : (a + 1) * 128, :].astype(F32)
-        center = jnp.mean(x, axis=-1, keepdims=True)
-        d = x - center
-        spread = jnp.mean(d * d, axis=-1, keepdims=True)
-        n = (d * lax.rsqrt(spread + EPSILON) * gain + shift).astype(BF16)
-        p = lax.dot_general(wt, n, (((1,), (1,)), ((), ())), preferred_element_type=F32)
-        left = jax.nn.sigmoid(p[0:128]) * p[128:256]
-        right = jax.nn.sigmoid(p[256:384]) * p[384:512]
-        scr_ref[pl.ds(a, 128, stride=16), :] = left
-        scr_ref[pl.ds(8 + a, 128, stride=16), :] = right
-        gate_ref[a * 128 : (a + 1) * 128, :] = jax.nn.sigmoid(
-            jnp.dot(n, wg, preferred_element_type=F32)
-        )
-    msg_ref[...] = scr_ref[...].astype(BF16)
+
+    def norm(t, carry):
+        pair_copy(t).wait()
+        for u in range(4):
+            rows = pl.ds(pl.multiple_of(t * 512 + u * 128, 128), 128)
+            x = pair_ref[rows, :].astype(F32)
+            center = jnp.mean(x, axis=-1, keepdims=True)
+            d = x - center
+            spread = jnp.mean(d * d, axis=-1, keepdims=True)
+            normed_ref[rows, :] = (d * lax.rsqrt(spread + EPSILON) * gain + shift).astype(BF16)
+        return carry
+
+    lax.fori_loop(0, 2, norm, 0)
+    w_copy.wait()
+    wt = jnp.transpose(w_ref[:, :512])
+    wg = w_ref[:, 512:640]
+
+    def step(t, carry):
+        for u in range(4):
+            a = t * 4 + u
+            rows = pl.ds(pl.multiple_of(a * 128, 128), 128)
+            n = normed_ref[rows, :]
+            p = lax.dot_general(wt, n, (((1,), (1,)), ((), ())), preferred_element_type=F32)
+            left = jax.nn.sigmoid(p[0:128]) * p[128:256]
+            right = jax.nn.sigmoid(p[256:384]) * p[384:512]
+            scr_ref[pl.ds(a, 128, stride=16), :] = left
+            scr_ref[pl.ds(8 + a, 128, stride=16), :] = right
+        return carry
+
+    lax.fori_loop(0, 2, step, 0)
+
+    def pack(t, carry):
+        rows = pl.ds(pl.multiple_of(t * 512, 512), 512)
+        msg_ref[rows, :] = scr_ref[rows, :].astype(BF16)
+        msg_copy(t).start()
+        return carry
+
+    lax.fori_loop(0, 4, pack, 0)
     small[2].wait()
     small[3].wait()
-    gain_col_ref[...] = jnp.transpose(jnp.broadcast_to(rows_ref[16:17, :], (128, 128)))
-    shift_col_ref[...] = jnp.transpose(jnp.broadcast_to(rows_ref[24:25, :], (128, 128)))
-    w_out_copy.wait()
+    for t in range(2):
+        rows = slice(t * 512, (t + 1) * 512)
+        gate_ref[rows, :] = jax.nn.sigmoid(
+            jnp.dot(normed_ref[rows, :], wg, preferred_element_type=F32)
+        )
+        if t == 1:
+            for k in range(2):
+                row = rows_ref[16 + 8 * k : 17 + 8 * k, :]
+                gate_ref[1024 + 128 * k : 1152 + 128 * k, :] = jnp.transpose(
+                    jnp.broadcast_to(row, (128, 128))
+                )
+        gate_copy(t, 512 + 256 * t).start()
+    for t in range(4):
+        msg_copy(t).wait()
+    for t in range(2):
+        gate_copy(t, 512 + 256 * t).wait()
 
 
 def spread_kernel(offset, recv_ref, out_ref):
@@ -154,12 +179,12 @@
     core = core_ref[0]
     multiply(left_ref, right_ref, mixed_ref)
     for q in range(8):
-        start = pl.multiple_of((2 * q + core) * 64, 64)
+        start = pl.multiple_of(((2 * q + core) ^ FLIP) * 64, 64)
         out_ref[pl.ds(start, 64), :] = own_ref[q * 64 : (q + 1) * 64, :]
-    pieces(mixed_ref, out_ref, lambda q: 2 * q + 1 - core)
-
-
-def output_kernel(recv_ref, gate_ref, gain_ref, shift_ref, w_ref, out_ref, scr_ref):
+    pieces(mixed_ref, out_ref, lambda q: (2 * q + 1 - core) ^ FLIP)
+
+
+def output_kernel(recv_ref, gate_ref, w_ref, out_ref, scr_ref):
     def total_step(t, sums):
         sums = list(sums)
         for u in range(16):
@@ -184,9 +209,11 @@
     spread = ((sums[0] + sums[1]) + (sums[2] + sums[3])) * (1.0 / 128.0)
     scale = lax.rsqrt(spread + EPSILON)
     w = w_ref[...]
+    gain = gate_ref[1024:1152, :]
+    shift = gate_ref[1152:1280, :]
     for s in range(8):
         x = scr_ref[pl.ds(s, 128, stride=8), :]
-        x = (x - center[s : s + 1]) * scale[s : s + 1] * gain_ref[...] + shift_ref[...]
+        x = (x - center[s : s + 1]) * scale[s : s + 1] * gain + shift
         o = lax.dot_general(
             x.astype(BF16), w, (((0,), (0,)), ((), ())), preferred_element_type=F32
         )
@@ -196,28 +223,40 @@
             out_ref[rows, :] = (gate_ref[rows, :] * o[b * 32 : (b + 1) * 32]).astype(BF16)
 
 
+def chip_groups():
+    groups = []
+    for core in range(2):
+        group = []
+        for a, b, c, d in itertools.product(range(2), range(8), range(2), range(4)):
+            xh, z, xl, y = a ^ ROOT[0], b ^ ROOT[1], c ^ ROOT[2], d ^ ROOT[3]
+            group.append((((xh * 8 + z) * 2 + xl) * 4 + y) * 2 + core)
+        groups.append(group)
+    return groups
+
+
+def exchange(x):
+    return lax.all_to_all(x, AXES, 0, 0, axis_index_groups=chip_groups(), tiled=True)
+
+
 def local(pair, norm_in, shift_in, in_weight, norm_out, shift_out, out_weight):
     core = lax.axis_index("core").astype(jnp.int32).reshape(1)
     shape = jax.ShapeDtypeStruct
-    msg, gate, gain_col, shift_col, w_out = pl.pallas_call(
+    msg, gate = pl.pallas_call(
         project_kernel,
-        out_shape=(
-            shape((2048, 128), BF16),
-            shape((1024, 128), F32),
-            shape((128, 128), F32),
-            shape((128, 128), F32),
-            shape((128, 128), BF16),
-        ),
-        in_specs=[HBM] * 7,
-        out_specs=(VMEM,) * 5,
+        out_shape=(shape((2048, 128), BF16), shape((1280, 128), F32)),
+        in_specs=[HBM] * 6,
+        out_specs=(HBM,) * 2,
         scratch_shapes=[
             pltpu.VMEM((1024, 128), BF16),
             pltpu.VMEM((128, 640), BF16),
             pltpu.VMEM((32, 128), F32),
+            pltpu.VMEM((1024, 128), BF16),
             pltpu.VMEM((2048, 128), F32),
-            pltpu.SemaphoreType.DMA((10,)),
+            pltpu.VMEM((2048, 128), BF16),
+            pltpu.VMEM((1280, 128), F32),
+            pltpu.SemaphoreType.DMA((7,)),
+            pltpu.SemaphoreType.DMA((6,)),
         ],
-        compiler_params=SMALL,
         name="project",
     )(
         pair.reshape(1024, 128),
@@ -226,9 +265,8 @@
         in_weight,
         norm_out.reshape(1, 128),
         shift_out.reshape(1, 128),
-        out_weight,
     )
-    recv = lax.all_to_all(msg.reshape(128, 16, 128), CHIPS, 0, 0, tiled=True).reshape(2048, 128)
+    recv = exchange(msg.reshape(128, 16, 128)).reshape(2048, 128)
     left = pl.pallas_call(
         functools.partial(spread_kernel, 0),
         out_shape=shape((512, 256), BF16),
@@ -257,16 +295,16 @@
         compiler_params=SMALL,
         name="other",
     )(core, other, right, own)
-    mixed = lax.all_to_all(back.reshape(128, 8, 128), CHIPS, 0, 0, tiled=True).reshape(1024, 128)
+    mixed = exchange(back.reshape(128, 8, 128)).reshape(1024, 128)
     out = pl.pallas_call(
         output_kernel,
         out_shape=shape((1024, 128), BF16),
-        in_specs=[VMEM] * 5,
+        in_specs=[VMEM] * 3,
         out_specs=VMEM,
         scratch_shapes=[pltpu.VMEM((1024, 128), F32)],
         compiler_params=SMALL,
         name="output",
-    )(mixed, gate, gain_col, shift_col, w_out)
+    )(mixed, gate, out_weight)
     return out.reshape(pair.shape)
 
 

time: 67.3 us -> 58.5 us (0.87)
  blocking collectives: 54.6 us -> 50.2 us
  local copies, waits for them, and re-layouts: 3.31 us -> 0.01 us
  starting transfers between devices: 2.78 us -> 1.19 us
    all_to_all x2, blocking collectives: 54.6 us -> 50.2 us  [exchange(): lax.all_to_all(x, AXES, 0, 0, axis_index_groups=chip_groups(), tiled=True)]
    unnamed x14 -> x4, local copies, waits for them, and re-layouts: 3.31 us -> 0.01 us
    ppermute x1, starting transfers between devices: 2.78 us -> 1.19 us  [local(): other = lax.ppermute(left, 'core', [(0, 1), (1, 0)])]
  transfers between devices with their start and end apart: 1 -> 1, of which waited for: 1 -> 1; matrix products, arithmetic and copies ran while one was open for 0% -> 0% of each run, Pallas kernels for 1% -> 2%
where the time goes in v4:
time: 58.5 us; the launch traced here: 58.3 us
  blocking collectives  50.2 us (86%)
  Pallas kernels  6.72 us (11%)
  starting transfers between devices  1.19 us (2%)
    all_to_all x2, blocking collectives, exchange(): lax.all_to_all(x, AXES, 0, 0, axis_index_groups=chip_groups(), tiled=True)  50.2 us
    pallas_call x1, Pallas kernels, local(): pl.pallas_call(project_kernel, out_shape=(shape((2048, 128), BF16), shape...  3.56 us
    ppermute x1, starting transfers between devices, local(): other = lax.ppermute(left, 'core', [(0, 1), (1, 0)])  1.19 us
  transfers between devices with their start and end apart: 1, of which 1 were waited for; matrix products, arithmetic and copies ran while one was open for 0% of the time, Pallas kernels for 2%

profile of v4, /device:TPU:1, one launch (start us, length us, event | category | flops | bytes accessed | tf_op | source)
XLA Modules:
  0.0 58.3 jit_solution(6626395317348592252)
XLA Ops:
  0.0 3.6 %project.1 = (bf16[2048,128]{1,0:T(8,128)(2,1)}, f32[1280,128]{1,0:T(8,128)}) custom-call(bf16[1024,128]{1,0:T(8,128)(2,1)} %bitcast.16, f32[1,128]{1,0:T(1,128)} %bitcast.17, f32[1,128]{1,0:T(1,128)} %bitcast.18, bf16[128,640]{1,0:T(8,128)(2,1)} %w_hbm.1, f32[1,128]{1,0:T(1,128)} %bitcast.19, f32[1,128]{1,0:T(1,128)} %bitcast.20), custom_call_target="tpu_custom_call" | custom-call | tf_op jit(solution)/shard_map/project/pallas_call | solution.py:244
  3.6 30.1 %all_to_all.10 = bf16[128,16,128]{2,1,0:T(8,128)(2,1)S(1)} all-to-all(bf16[128,16,128]{2,1,0:T(8,128)(2,1)} %bitcast.15), channel_id=1, replica_groups={{196,198,192,194,204,206,200,202,212,214,208,210,220,222,216,218,228,23..., dimensions={0} | all-to-all | bytes 1048576 | tf_op jit(solution)/shard_map/all_to_all | solution.py:238
  33.7 0.4 spread.1.left_ref
  34.1 1.2 %collective-permute-start = (bf16[512,256]{1,0:T(8,128)(2,1)S(1)}, bf16[512,256]{1,0:T(8,128)(2,1)S(1)}, u32[]{:S(2)}, u32[]{:S(2)}) collective-permute-start(bf16[512,256]{1,0:T(8,128)(2,1)S(1)} %spread.1.left_ref), channel_id=1, source_target_pairs={{0,1},{1,0},{2,3},{3,2},{4,5},{5,4},{6,7},{7,6},{8,9},{9,8},{10,11... | collective-permute-start | bytes 786440 | tf_op jit(solution)/shard_map/ppermute | solution.py:278
  35.3 1.0 %own.1 = (bf16[512,256]{1,0:T(8,128)(2,1)S(1)}, bf16[512,128]{1,0:T(8,128)(2,1)S(1)}) custom-call(bf16[2048,128]{1,0:T(8,128)(2,1)S(1)} %bitcast.12, bf16[512,256]{1,0:T(8,128)(2,1)S(1)} %spread.1.left_ref), custom_call_target="tpu_custom_call" | custom-call | flops 67108864 | bytes 1048576 | tf_op jit(solution)/shard_map/own/pallas_call | solution.py:279
  36.3 0.2 collective-permute-done.left_ref
  36.5 0.0 copy-start
  36.5 0.6 %other.1 = bf16[1024,128]{1,0:T(8,128)(2,1)S(1)} custom-call(s32[1]{0:T(128)} %bitcast.core_ref, bf16[512,256]{1,0:T(8,128)(2,1)S(1)} %collective-permute-done.left_ref, bf16[512,256]{1,0:T(8,128)(2,1)S(1)} %get-tuple-element.10.right_ref, bf16[512,128]{1,0:T(8,128)(2,1)S(1)} %get-tuple-element.11.own_ref), custom_call_target="tpu_custom_call" | custom-call | tf_op jit(solution)/shard_map/other/pallas_call | solution.py:289
  37.1 0.0 copy-start.1
  37.1 20.0 %all_to_all.11 = bf16[128,8,128]{2,1,0:T(8,128)(2,1)S(1)} all-to-all(bf16[128,8,128]{2,1,0:T(8,128)(2,1)S(1)} %bitcast.13), channel_id=1, replica_groups={{196,198,192,194,204,206,200,202,212,214,208,210,220,222,216,218,228,23..., dimensions={0} | all-to-all | bytes 524288 | tf_op jit(solution)/shard_map/all_to_all | solution.py:238
  57.1 0.0 copy-done
  57.1 0.0 copy-done.1
  57.1 1.2 %output.1 = bf16[1024,128]{1,0:T(8,128)(2,1)} custom-call(bf16[1024,128]{1,0:T(8,128)(2,1)S(1)} %bitcast.14, f32[1280,128]{1,0:T(8,128)S(1)} %copy-done, bf16[128,128]{1,0:T(8,128)(2,1)S(1)} %copy-done.1), custom_call_target="tpu_custom_call" | custom-call | tf_op jit(solution)/shard_map/output/pallas_call | solution.py:299
Async XLA Ops:
  34.1 2.3 %collective-permute-start = (bf16[512,256]{1,0:T(8,128)(2,1)S(1)}, bf16[512,256]{1,0:T(8,128)(2,1)S(1)}, u32[]{:S(2)}, u32[]{:S(2)}) collective-permute-start(bf16[512,256]{1,0:T(8,128)(2,1)S(1)} %spread.1.left_ref), channel_id=1, source_target_pairs={{0,1},{1,0},{2,3},{3,2},{4,5},{5,4},{6,7},{7,6},{8,9},{9,8},{10,11... | collective-permute-start | bytes 786440 | tf_op jit(solution)/shard_map/ppermute | solution.py:278
  36.5 20.6 %copy-start = (f32[1280,128]{1,0:T(8,128)S(1)}, f32[1280,128]{1,0:T(8,128)}, u32[]{:S(2)}) copy-start(f32[1280,128]{1,0:T(8,128)} %get-tuple-element.12.gate_ref) | copy-start | bytes 1966084
  37.1 20.0 %copy-start.1 = (bf16[128,128]{1,0:T(8,128)(2,1)S(1)}, bf16[128,128]{1,0:T(8,128)(2,1)}, u32[]{:S(2)}) copy-start(bf16[128,128]{1,0:T(8,128)(2,1)} %w_ref.1) | copy-start | bytes 98308

commit v5 on v4

--- a/solution.py
+++ b/solution.py
@@ -39,26 +39,20 @@
 
 
 def project_kernel(
-    pair_hbm, gain_hbm, shift_hbm, w_hbm, gain_out_hbm, shift_out_hbm, msg_hbm, gate_hbm,
-    pair_ref, w_ref, rows_ref, normed_ref, scr_ref, msg_ref, gate_ref, sem, out_sem,
+    pair_hbm, gain_hbm, shift_hbm, w_hbm, gain_out_hbm, shift_out_hbm,
+    msg_ref, normed_ref, aux_ref, w_gate_ref,
+    pair_ref, w_ref, rows_ref, scr_ref, sem,
 ):
     def pair_copy(t):
         rows = pl.ds(t * 512, 512)
-        return pltpu.make_async_copy(pair_hbm.at[rows], pair_ref.at[rows], sem.at[5 + t])
-
-    def gate_copy(t, size):
-        rows = pl.ds(t * 512, size)
-        return pltpu.make_async_copy(gate_ref.at[rows], gate_hbm.at[rows], out_sem.at[4 + t])
-
-    def msg_copy(t):
-        rows = pl.ds(t * 512, 512)
-        return pltpu.make_async_copy(msg_ref.at[rows], msg_hbm.at[rows], out_sem.at[t])
+        return pltpu.make_async_copy(pair_hbm.at[rows], pair_ref.at[rows], sem.at[6 + t])
 
     small = [
         pltpu.make_async_copy(ref, rows_ref.at[pl.ds(t * 8, 1)], sem.at[t])
         for t, ref in enumerate((gain_hbm, shift_hbm, gain_out_hbm, shift_out_hbm))
     ]
-    w_copy = pltpu.make_async_copy(w_hbm, w_ref, sem.at[4])
+    w_copy = pltpu.make_async_copy(w_hbm.at[:, pl.ds(0, 512)], w_ref, sem.at[4])
+    w_gate_copy = pltpu.make_async_copy(w_hbm.at[:, pl.ds(512, 128)], w_gate_ref, sem.at[5])
     small[0].start()
     small[1].start()
     pair_copy(0).start()
@@ -66,6 +60,7 @@
     w_copy.start()
     small[2].start()
     small[3].start()
+    w_gate_copy.start()
     small[0].wait()
     small[1].wait()
     gain = rows_ref[0:1, :]
@@ -84,19 +79,19 @@
 
     lax.fori_loop(0, 2, norm, 0)
     w_copy.wait()
-    wt = jnp.transpose(w_ref[:, :512])
-    wg = w_ref[:, 512:640]
+    wt = jnp.transpose(w_ref[...])
 
     def step(t, carry):
-        for u in range(4):
-            a = t * 4 + u
-            rows = pl.ds(pl.multiple_of(a * 128, 128), 128)
-            n = normed_ref[rows, :]
+        for u in range(2):
+            n = normed_ref[pl.ds(pl.multiple_of(t * 512 + u * 256, 256), 256), :]
             p = lax.dot_general(wt, n, (((1,), (1,)), ((), ())), preferred_element_type=F32)
             left = jax.nn.sigmoid(p[0:128]) * p[128:256]
             right = jax.nn.sigmoid(p[256:384]) * p[384:512]
-            scr_ref[pl.ds(a, 128, stride=16), :] = left
-            scr_ref[pl.ds(8 + a, 128, stride=16), :] = right
+            for k in range(2):
+                a = t * 4 + u * 2 + k
+                lanes = slice(k * 128, (k + 1) * 128)
+                scr_ref[pl.ds(a, 128, stride=16), :] = left[:, lanes]
+                scr_ref[pl.ds(8 + a, 128, stride=16), :] = right[:, lanes]
         return carry
 
     lax.fori_loop(0, 2, step, 0)
@@ -104,28 +99,14 @@
     def pack(t, carry):
         rows = pl.ds(pl.multiple_of(t * 512, 512), 512)
         msg_ref[rows, :] = scr_ref[rows, :].astype(BF16)
-        msg_copy(t).start()
         return carry
 
     lax.fori_loop(0, 4, pack, 0)
     small[2].wait()
     small[3].wait()
-    for t in range(2):
-        rows = slice(t * 512, (t + 1) * 512)
-        gate_ref[rows, :] = jax.nn.sigmoid(
-            jnp.dot(normed_ref[rows, :], wg, preferred_element_type=F32)
-        )
-        if t == 1:
-            for k in range(2):
-                row = rows_ref[16 + 8 * k : 17 + 8 * k, :]
-                gate_ref[1024 + 128 * k : 1152 + 128 * k, :] = jnp.transpose(
-                    jnp.broadcast_to(row, (128, 128))
-                )
-        gate_copy(t, 512 + 256 * t).start()
-    for t in range(4):
-        msg_copy(t).wait()
-    for t in range(2):
-        gate_copy(t, 512 + 256 * t).wait()
+    aux_ref[0:1, :] = rows_ref[16:17, :]
+    aux_ref[8:9, :] = rows_ref[24:25, :]
+    w_gate_copy.wait()
 
 
 def spread_kernel(offset, recv_ref, out_ref):
@@ -169,10 +150,19 @@
     lax.fori_loop(0, 2, step, 0)
 
 
-def own_kernel(recv_ref, left_ref, right_ref, out_ref, mixed_ref):
+def own_kernel(
+    recv_ref, left_ref, normed_ref, aux_ref, w_gate_ref, right_ref, out_ref, gate_ref, mixed_ref
+):
     spread_kernel(8, recv_ref, right_ref)
     multiply(left_ref, right_ref, mixed_ref)
+    gate_ref[0:1024, :] = jax.nn.sigmoid(
+        jnp.dot(normed_ref[...], w_gate_ref[...], preferred_element_type=F32)
+    )
     pieces(mixed_ref, out_ref, lambda q: q)
+    for k in range(2):
+        gate_ref[1024 + 128 * k : 1152 + 128 * k, :] = jnp.transpose(
+            jnp.broadcast_to(aux_ref[8 * k : 8 * k + 1, :], (128, 128))
+        )
 
 
 def other_kernel(core_ref, left_ref, right_ref, own_ref, out_ref, mixed_ref):
@@ -241,30 +231,33 @@
 def local(pair, norm_in, shift_in, in_weight, norm_out, shift_out, out_weight):
     core = lax.axis_index("core").astype(jnp.int32).reshape(1)
     shape = jax.ShapeDtypeStruct
-    msg, gate = pl.pallas_call(
+    stay = functools.partial(pltpu.with_memory_space_constraint, memory_space=pltpu.HBM)
+    msg, normed, aux, w_gate = pl.pallas_call(
         project_kernel,
-        out_shape=(shape((2048, 128), BF16), shape((1280, 128), F32)),
+        out_shape=(
+            shape((2048, 128), BF16),
+            shape((1024, 128), BF16),
+            shape((16, 128), F32),
+            shape((128, 128), BF16),
+        ),
         in_specs=[HBM] * 6,
-        out_specs=(HBM,) * 2,
+        out_specs=(VMEM,) * 4,
         scratch_shapes=[
             pltpu.VMEM((1024, 128), BF16),
-            pltpu.VMEM((128, 640), BF16),
+            pltpu.VMEM((128, 512), BF16),
             pltpu.VMEM((32, 128), F32),
-            pltpu.VMEM((1024, 128), BF16),
             pltpu.VMEM((2048, 128), F32),
-            pltpu.VMEM((2048, 128), BF16),
-            pltpu.VMEM((1280, 128), F32),
-            pltpu.SemaphoreType.DMA((7,)),
-            pltpu.SemaphoreType.DMA((6,)),
+            pltpu.SemaphoreType.DMA((8,)),
         ],
+        compiler_params=SMALL,
         name="project",
     )(
-        pair.reshape(1024, 128),
-        norm_in.reshape(1, 128),
-        shift_in.reshape(1, 128),
-        in_weight,
-        norm_out.reshape(1, 128),
-        shift_out.reshape(1, 128),
+        stay(pair.reshape(1024, 128)),
+        stay(norm_in.reshape(1, 128)),
+        stay(shift_in.reshape(1, 128)),
+        stay(in_weight),
+        stay(norm_out.reshape(1, 128)),
+        stay(shift_out.reshape(1, 128)),
     )
     recv = exchange(msg.reshape(128, 16, 128)).reshape(2048, 128)
     left = pl.pallas_call(
@@ -276,16 +269,16 @@
         name="spread",
     )(recv)
     other = lax.ppermute(left, "core", [(0, 1), (1, 0)])
-    right, own = pl.pallas_call(
+    right, own, gate = pl.pallas_call(
         own_kernel,
-        out_shape=(shape((512, 256), BF16), shape((512, 128), BF16)),
-        in_specs=[VMEM, VMEM],
-        out_specs=(VMEM, VMEM),
+        out_shape=(shape((512, 256), BF16), shape((512, 128), BF16), shape((1280, 128), F32)),
+        in_specs=[VMEM] * 5,
+        out_specs=(VMEM,) * 3,
         scratch_shapes=[pltpu.VMEM((256, 256), F32)],
         compiler_params=SMALL,
         name="own",
         cost_estimate=pl.CostEstimate(flops=1 << 26, bytes_accessed=1 << 20, transcendentals=0),
-    )(recv, left)
+    )(recv, left, normed, aux, w_gate)
     back = pl.pallas_call(
         other_kernel,
         out_shape=shape((1024, 128), BF16),

time: 58.5 us -> 57.1 us (0.976)
  Pallas kernels: 6.72 us -> 5.66 us
    pallas_call x1, Pallas kernels: 3.56 us -> 2.37 us  [local(): pl.pallas_call(project_kernel, out_shape=(shape((2048, 128), BF16), shape...]
  transfers between devices with their start and end apart: 1 -> 1, of which waited for: 1 -> 0; matrix products, arithmetic and copies ran while one was open for 0% -> 0% of each run, Pallas kernels for 2% -> 2%
where the time goes in v5:
time: 57.1 us; the launch traced here: 56.9 us
  blocking collectives  49.9 us (87%)
  Pallas kernels  5.66 us (10%)
  starting transfers between devices  1.19 us (2%)
    all_to_all x2, blocking collectives, exchange(): lax.all_to_all(x, AXES, 0, 0, axis_index_groups=chip_groups(), tiled=True)  49.9 us
    pallas_call x1, Pallas kernels, local(): pl.pallas_call(project_kernel, out_shape=(shape((2048, 128), BF16), shape...  2.37 us
    ppermute x1, starting transfers between devices, local(): other = lax.ppermute(left, 'core', [(0, 1), (1, 0)])  1.19 us
    pallas_call x1, Pallas kernels, local(): pl.pallas_call(output_kernel, out_shape=shape((1024, 128), BF16), in_spec...  1.15 us
  transfers between devices with their start and end apart: 1, of which 0 were waited for; matrix products, arithmetic and copies ran while one was open for 0% of the time, Pallas kernels for 2%

profile of v5, /device:TPU:1, one launch (start us, length us, event | category | flops | bytes accessed | tf_op | source)
XLA Modules:
  0.0 56.9 jit_solution(6752608910686882900)
XLA Ops:
  0.0 2.4 %project.1 = (bf16[2048,128]{1,0:T(8,128)(2,1)S(1)}, bf16[1024,128]{1,0:T(8,128)(2,1)S(1)}, f32[16,128]{1,0:T(8,128)S(1)}, bf16[128,128]{1,0:T(8,128)(2,1)S(1)}) custom-call(bf16[1024,128]{1,0:T(8,128)(2,1)} %bitcast.16, f32[1,128]{1,0:T(1,128)} %bitcast.17, f32[1,128]{1,0:T(1,128)} %bitcast.18, bf16[128,640]{1,0:T(8,128)(2,1)} %w_hbm.1, f32[1,128]{1,0:T(1,128)} %bitcast.19, ...), custom_call_target="tpu_custom_call" | custom-call | tf_op jit(solution)/shard_map/project/pallas_call | solution.py:235
  2.4 29.9 %all_to_all.10 = bf16[128,16,128]{2,1,0:T(8,128)(2,1)S(1)} all-to-all(bf16[128,16,128]{2,1,0:T(8,128)(2,1)S(1)} %bitcast.15), channel_id=1, replica_groups={{196,198,192,194,204,206,200,202,212,214,208,210,220,222,216,218,228,23..., dimensions={0} | all-to-all | bytes 1048576 | tf_op jit(solution)/shard_map/all_to_all | solution.py:228
  32.3 0.4 spread.1.left_ref
  32.7 1.2 %collective-permute-start = (bf16[512,256]{1,0:T(8,128)(2,1)S(1)}, bf16[512,256]{1,0:T(8,128)(2,1)S(1)}, u32[]{:S(2)}, u32[]{:S(2)}) collective-permute-start(bf16[512,256]{1,0:T(8,128)(2,1)S(1)} %spread.1.left_ref), channel_id=1, source_target_pairs={{0,1},{1,0},{2,3},{3,2},{4,5},{5,4},{6,7},{7,6},{8,9},{9,8},{10,11... | collective-permute-start | bytes 786440 | tf_op jit(solution)/shard_map/ppermute | solution.py:271
  33.9 1.1 %own.1 = (bf16[512,256]{1,0:T(8,128)(2,1)S(1)}, bf16[512,128]{1,0:T(8,128)(2,1)S(1)}, f32[1280,128]{1,0:T(8,128)S(1)}) custom-call(bf16[2048,128]{1,0:T(8,128)(2,1)S(1)} %bitcast.12, bf16[512,256]{1,0:T(8,128)(2,1)S(1)} %spread.1.left_ref, bf16[1024,128]{1,0:T(8,128)(2,1)S(1)} %get-tuple-element.13.normed_ref, f32[16,128]{1,0:T(8,128)S(1)} %get-tuple-element.14.aux_ref, ...), custom_call_target="tpu_custom_call" | custom-call | flops 67108864 | bytes 1048576 | tf_op jit(solution)/shard_map/own/pallas_call | solution.py:272
  35.0 0.0 collective-permute-done.left_ref
  35.1 0.6 %other.1 = bf16[1024,128]{1,0:T(8,128)(2,1)S(1)} custom-call(s32[1]{0:T(128)} %bitcast.core_ref, bf16[512,256]{1,0:T(8,128)(2,1)S(1)} %collective-permute-done.left_ref, bf16[512,256]{1,0:T(8,128)(2,1)S(1)} %get-tuple-element.16.right_ref, bf16[512,128]{1,0:T(8,128)(2,1)S(1)} %get-tuple-element.17.own_ref), custom_call_target="tpu_custom_call" | custom-call | tf_op jit(solution)/shard_map/other/pallas_call | solution.py:282
  35.7 0.0 copy-start
  35.7 20.0 %all_to_all.11 = bf16[128,8,128]{2,1,0:T(8,128)(2,1)S(1)} all-to-all(bf16[128,8,128]{2,1,0:T(8,128)(2,1)S(1)} %bitcast.13), channel_id=1, replica_groups={{196,198,192,194,204,206,200,202,212,214,208,210,220,222,216,218,228,23..., dimensions={0} | all-to-all | bytes 524288 | tf_op jit(solution)/shard_map/all_to_all | solution.py:228
  55.7 0.0 copy-done
  55.7 1.2 %output.1 = bf16[1024,128]{1,0:T(8,128)(2,1)} custom-call(bf16[1024,128]{1,0:T(8,128)(2,1)S(1)} %bitcast.14, f32[1280,128]{1,0:T(8,128)S(1)} %get-tuple-element.18.gate_ref, bf16[128,128]{1,0:T(8,128)(2,1)S(1)} %copy-done), custom_call_target="tpu_custom_call" | custom-call | tf_op jit(solution)/shard_map/output/pallas_call | solution.py:292
Async XLA Ops:
  32.7 2.3 %collective-permute-start = (bf16[512,256]{1,0:T(8,128)(2,1)S(1)}, bf16[512,256]{1,0:T(8,128)(2,1)S(1)}, u32[]{:S(2)}, u32[]{:S(2)}) collective-permute-start(bf16[512,256]{1,0:T(8,128)(2,1)S(1)} %spread.1.left_ref), channel_id=1, source_target_pairs={{0,1},{1,0},{2,3},{3,2},{4,5},{5,4},{6,7},{7,6},{8,9},{9,8},{10,11... | collective-permute-start | bytes 786440 | tf_op jit(solution)/shard_map/ppermute | solution.py:271
  35.7 20.0 %copy-start = (bf16[128,128]{1,0:T(8,128)(2,1)S(1)}, bf16[128,128]{1,0:T(8,128)(2,1)}, u32[]{:S(2)}) copy-start(bf16[128,128]{1,0:T(8,128)(2,1)} %w_ref.1) | copy-start | bytes 98308

commit v6 on v5

--- a/solution.py
+++ b/solution.py
@@ -11,13 +11,24 @@
 EPSILON = 1e-05
 AXES = ("xh", "z", "xl", "y", "core")
 ROOT = (1, 4, 0, 2)
-FLIP = (8 * ROOT[0] + ROOT[1]) ^ (8 * ROOT[2] + 2 * ROOT[3])
+
+
+def hops(p, q):
+    def ring(a, b, n):
+        return min((a - b) % n, (b - a) % n)
+
+    x = ring(2 * p[0] + p[2], 2 * q[0] + q[2], 4)
+    return x + ring(p[1], q[1], 8) + ring(p[3], q[3], 4)
+
+
+CHIPS = list(itertools.product(range(2), range(8), range(2), range(4)))
+CHIPS.sort(key=lambda p: (p != ROOT, -hops(p, ROOT), p))
+MEMBER = {p: n for n, p in enumerate(CHIPS)}
 F32 = jnp.float32
 BF16 = jnp.bfloat16
 VMEM = pl.BlockSpec(memory_space=pltpu.VMEM)
 SMEM = pl.BlockSpec(memory_space=pltpu.SMEM)
 HBM = pl.BlockSpec(memory_space=pltpu.HBM)
-UNROLL = 8
 SMALL = pltpu.CompilerParams(vmem_limit_bytes=12 << 20)
 
 
@@ -77,9 +88,10 @@
             normed_ref[rows, :] = (d * lax.rsqrt(spread + EPSILON) * gain + shift).astype(BF16)
         return carry
 
-    lax.fori_loop(0, 2, norm, 0)
+    norm(0, 0)
     w_copy.wait()
     wt = jnp.transpose(w_ref[...])
+    norm(1, 0)
 
     def step(t, carry):
         for u in range(2):
@@ -94,7 +106,8 @@
                 scr_ref[pl.ds(8 + a, 128, stride=16), :] = right[:, lanes]
         return carry
 
-    lax.fori_loop(0, 2, step, 0)
+    for t in range(2):
+        step(t, 0)
 
     def pack(t, carry):
         rows = pl.ds(pl.multiple_of(t * 512, 512), 512)
@@ -110,22 +123,22 @@
 
 
 def spread_kernel(offset, recv_ref, out_ref):
-    def step(t, carry):
-        for u in range(UNROLL):
-            r = t * UNROLL + u
-            for g in range(2):
-                base = r * 128 + g * 64
+    def step(xh, carry):
+        for z in range(8):
+            for xl in range(2):
                 v = []
-                for c in range(4):
-                    start = pl.multiple_of(base + c * 16, 16)
+                for y in range(4):
+                    low, high = (MEMBER[(t, z, xl, y)] for t in range(2))
+                    start = pl.multiple_of((low + xh * (high - low)) * 16, 16)
                     piece = recv_ref[pl.ds(start, 16), :].astype(F32)
                     v.append(piece[offset : offset + 8])
-                out_ref[pl.ds(pl.multiple_of(r * 32, 32), 32), g * 128 : (g + 1) * 128] = (
-                    jnp.concatenate(swap_groups(v), axis=0).astype(BF16)
-                )
-        return carry
-
-    lax.fori_loop(0, 16 // UNROLL, step, 0)
+                start = pl.multiple_of((xh * 8 + z) * 32, 32)
+                out_ref[pl.ds(start, 32), xl * 128 : (xl + 1) * 128] = jnp.concatenate(
+                    swap_groups(v), axis=0
+                ).astype(BF16)
+        return carry
+
+    lax.fori_loop(0, 2, step, 0)
 
 
 def multiply(left_ref, right_ref, mixed_ref):
@@ -134,17 +147,20 @@
     )
 
 
-def pieces(mixed_ref, out_ref, row_of):
-    def step(t, carry):
-        for u in range(4):
-            q = t * 4 + u
+def member(xh, y, core, chip):
+    a, b, c, d = (MEMBER[(t, 2 * y + u, *chip)] for t in range(2) for u in range(2))
+    return a + xh * (c - a) + core * ((b - a) + xh * (a - b - c + d))
+
+
+def pieces(mixed_ref, store):
+    def step(xl, carry):
+        for y in range(4):
             for g in range(2):
                 v = []
                 for b in range(4):
-                    start = pl.multiple_of(q * 32 + b * 8, 8)
+                    start = pl.multiple_of((xl * 4 + y) * 32 + b * 8, 8)
                     v.append(mixed_ref[pl.ds(start, 8), g * 128 : (g + 1) * 128])
-                start = pl.multiple_of(row_of(q) * 64 + g * 32, 32)
-                out_ref[pl.ds(start, 32), :] = jnp.concatenate(swap_groups(v), axis=0).astype(BF16)
+                store(xl, y, g, swap_groups(v))
         return carry
 
     lax.fori_loop(0, 2, step, 0)
@@ -158,7 +174,12 @@
     gate_ref[0:1024, :] = jax.nn.sigmoid(
         jnp.dot(normed_ref[...], w_gate_ref[...], preferred_element_type=F32)
     )
-    pieces(mixed_ref, out_ref, lambda q: q)
+
+    def store(xl, y, g, v):
+        start = pl.multiple_of(((xl * 4 + y) * 2 + g) * 32, 32)
+        out_ref[pl.ds(start, 32), :] = jnp.concatenate(v, axis=0).astype(BF16)
+
+    pieces(mixed_ref, store)
     for k in range(2):
         gate_ref[1024 + 128 * k : 1152 + 128 * k, :] = jnp.transpose(
             jnp.broadcast_to(aux_ref[8 * k : 8 * k + 1, :], (128, 128))
@@ -168,34 +189,46 @@
 def other_kernel(core_ref, left_ref, right_ref, own_ref, out_ref, mixed_ref):
     core = core_ref[0]
     multiply(left_ref, right_ref, mixed_ref)
-    for q in range(8):
-        start = pl.multiple_of(((2 * q + core) ^ FLIP) * 64, 64)
-        out_ref[pl.ds(start, 64), :] = own_ref[q * 64 : (q + 1) * 64, :]
-    pieces(mixed_ref, out_ref, lambda q: (2 * q + 1 - core) ^ FLIP)
-
-
-def output_kernel(recv_ref, gate_ref, w_ref, out_ref, scr_ref):
+
+    def store(xl, y, g, v):
+        for c in range(4):
+            start = pl.multiple_of((xl * 4 + y) * 64 + (g * 4 + c) * 8, 8)
+            out_ref[member(xl, y, core, (g, c))] = own_ref[pl.ds(start, 8), :]
+            out_ref[member(xl, y, 1 - core, (g, c))] = v[c].astype(BF16)
+
+    pieces(mixed_ref, store)
+
+
+def output_kernel(recv_ref, gate_ref, w_ref, out_hbm, scr_ref, out_ref, sem):
+    def out_copy(half, b):
+        rows = pl.ds((b * 8 + half * 4) * 32, 128)
+        return pltpu.make_async_copy(out_ref.at[rows], out_hbm.at[rows], sem.at[half * 4 + b])
+
     def total_step(t, sums):
         sums = list(sums)
         for u in range(16):
-            rows = pl.ds(pl.multiple_of(t * 256 + u * 16, 16), 16)
+            rows = pl.ds(t * 256 + u * 16, 16)
             x = recv_ref[rows, :].astype(F32)
             scr_ref[rows, :] = x
             sums[u % 4] = sums[u % 4] + (x[0:8] + x[8:16])
         return tuple(sums)
 
     zero = jnp.zeros((8, 128), F32)
-    sums = lax.fori_loop(0, 4, total_step, (zero,) * 4)
+    sums = (zero,) * 4
+    for t in range(4):
+        sums = total_step(t, sums)
     center = ((sums[0] + sums[1]) + (sums[2] + sums[3])) * (1.0 / 128.0)
 
     def square_step(t, sums):
         sums = list(sums)
         for u in range(32):
-            d = scr_ref[pl.ds(pl.multiple_of(t * 256 + u * 8, 8), 8), :] - center
+            d = scr_ref[pl.ds(t * 256 + u * 8, 8), :] - center
             sums[u % 4] = sums[u % 4] + d * d
         return tuple(sums)
 
-    sums = lax.fori_loop(0, 4, square_step, (zero,) * 4)
+    sums = (zero,) * 4
+    for t in range(4):
+        sums = square_step(t, sums)
     spread = ((sums[0] + sums[1]) + (sums[2] + sums[3])) * (1.0 / 128.0)
     scale = lax.rsqrt(spread + EPSILON)
     w = w_ref[...]
@@ -211,17 +244,19 @@
             i = b * 8 + s
             rows = slice(i * 32, (i + 1) * 32)
             out_ref[rows, :] = (gate_ref[rows, :] * o[b * 32 : (b + 1) * 32]).astype(BF16)
+        if s % 4 == 3:
+            for b in range(4):
+                out_copy(s // 4, b).start()
+    for half in range(2):
+        for b in range(4):
+            out_copy(half, b).wait()
 
 
 def chip_groups():
-    groups = []
-    for core in range(2):
-        group = []
-        for a, b, c, d in itertools.product(range(2), range(8), range(2), range(4)):
-            xh, z, xl, y = a ^ ROOT[0], b ^ ROOT[1], c ^ ROOT[2], d ^ ROOT[3]
-            group.append((((xh * 8 + z) * 2 + xl) * 4 + y) * 2 + core)
-        groups.append(group)
-    return groups
+    return [
+        [(((xh * 8 + z) * 2 + xl) * 4 + y) * 2 + core for xh, z, xl, y in CHIPS]
+        for core in range(2)
+    ]
 
 
 def exchange(x):
@@ -281,20 +316,24 @@
     )(recv, left, normed, aux, w_gate)
     back = pl.pallas_call(
         other_kernel,
-        out_shape=shape((1024, 128), BF16),
+        out_shape=shape((128, 8, 128), BF16),
         in_specs=[SMEM, VMEM, VMEM, VMEM],
         out_specs=VMEM,
         scratch_shapes=[pltpu.VMEM((256, 256), F32)],
         compiler_params=SMALL,
         name="other",
     )(core, other, right, own)
-    mixed = exchange(back.reshape(128, 8, 128)).reshape(1024, 128)
+    mixed = exchange(back).reshape(1024, 128)
     out = pl.pallas_call(
         output_kernel,
         out_shape=shape((1024, 128), BF16),
         in_specs=[VMEM] * 3,
-        out_specs=VMEM,
-        scratch_shapes=[pltpu.VMEM((1024, 128), F32)],
+        out_specs=HBM,
+        scratch_shapes=[
+            pltpu.VMEM((1024, 128), F32),
+            pltpu.VMEM((1024, 128), BF16),
+            pltpu.SemaphoreType.DMA((8,)),
+        ],
         compiler_params=SMALL,
         name="output",
     )(mixed, gate, out_weight)

time: 57.1 us -> 56.2 us (0.984)
  blocking collectives: 49.9 us -> 48.8 us
    all_to_all x2, blocking collectives: 49.9 us -> 48.8 us  [exchange(): lax.all_to_all(x, AXES, 0, 0, axis_index_groups=chip_groups(), tiled=True)]
where the time goes in v6:
time: 56.2 us; the launch traced here: 56 us
  blocking collectives  48.8 us (87%)
  Pallas kernels  5.47 us (10%)
  starting transfers between devices  1.63 us (3%)
    all_to_all x2, blocking collectives, exchange(): lax.all_to_all(x, AXES, 0, 0, axis_index_groups=chip_groups(), tiled=True)  48.8 us
    pallas_call x1, Pallas kernels, local(): pl.pallas_call(project_kernel, out_shape=(shape((2048, 128), BF16), shape...  2.09 us
    ppermute x1, starting transfers between devices, local(): other = lax.ppermute(left, 'core', [(0, 1), (1, 0)])  1.63 us
    pallas_call x1, Pallas kernels, local(): pl.pallas_call(own_kernel, out_shape=(shape((512, 256), BF16), shape((512...  1.15 us
    pallas_call x1, Pallas kernels, local(): pl.pallas_call(output_kernel, out_shape=shape((1024, 128), BF16), in_spec...  1.13 us
  transfers between devices with their start and end apart: 1, of which 0 were waited for; matrix products, arithmetic and copies ran while one was open for 0% of the time, Pallas kernels for 2%

profile of v6, /device:TPU:1, one launch (start us, length us, event | category | flops | bytes accessed | tf_op | source)
XLA Modules:
  0.0 56.0 jit_solution(5578028446336165595)
XLA Ops:
  0.0 2.1 %project.1 = (bf16[2048,128]{1,0:T(8,128)(2,1)S(1)}, bf16[1024,128]{1,0:T(8,128)(2,1)S(1)}, f32[16,128]{1,0:T(8,128)S(1)}, bf16[128,128]{1,0:T(8,128)(2,1)S(1)}) custom-call(bf16[1024,128]{1,0:T(8,128)(2,1)} %bitcast.14, f32[1,128]{1,0:T(1,128)} %bitcast.15, f32[1,128]{1,0:T(1,128)} %bitcast.16, bf16[128,640]{1,0:T(8,128)(2,1)} %w_hbm.1, f32[1,128]{1,0:T(1,128)} %bitcast.17, ...), custom_call_target="tpu_custom_call" | custom-call | tf_op jit(solution)/shard_map/project/pallas_call | solution.py:270
  2.1 29.5 %all_to_all.10 = bf16[128,16,128]{2,1,0:T(8,128)(2,1)S(1)} all-to-all(bf16[128,16,128]{2,1,0:T(8,128)(2,1)S(1)} %bitcast.13), channel_id=1, replica_groups={{196,0,2,6,8,16,112,136,4,10,14,18,22,24,32,96,114,118,120,128,138,142,..., dimensions={0} | all-to-all | bytes 1048576 | tf_op jit(solution)/shard_map/all_to_all | solution.py:263
  31.6 0.4 spread.1.left_ref
  32.1 1.6 %collective-permute-start = (bf16[512,256]{1,0:T(8,128)(2,1)S(1)}, bf16[512,256]{1,0:T(8,128)(2,1)S(1)}, u32[]{:S(2)}, u32[]{:S(2)}) collective-permute-start(bf16[512,256]{1,0:T(8,128)(2,1)S(1)} %spread.1.left_ref), channel_id=1, source_target_pairs={{0,1},{1,0},{2,3},{3,2},{4,5},{5,4},{6,7},{7,6},{8,9},{9,8},{10,11... | collective-permute-start | bytes 786440 | tf_op jit(solution)/shard_map/ppermute | solution.py:306
  33.7 1.2 %own.1 = (bf16[512,256]{1,0:T(8,128)(2,1)S(1)}, bf16[512,128]{1,0:T(8,128)(2,1)S(1)}, f32[1280,128]{1,0:T(8,128)S(1)}) custom-call(bf16[2048,128]{1,0:T(8,128)(2,1)S(1)} %bitcast.11, bf16[512,256]{1,0:T(8,128)(2,1)S(1)} %spread.1.left_ref, bf16[1024,128]{1,0:T(8,128)(2,1)S(1)} %get-tuple-element.13.normed_ref, f32[16,128]{1,0:T(8,128)S(1)} %get-tuple-element.14.aux_ref, ...), custom_call_target="tpu_custom_call" | custom-call | flops 67108864 | bytes 1048576 | tf_op jit(solution)/shard_map/own/pallas_call | solution.py:307
  34.9 0.0 collective-permute-done.left_ref
  34.9 0.7 %other.1 = bf16[128,8,128]{2,1,0:T(8,128)(2,1)S(1)} custom-call(s32[1]{0:T(128)} %bitcast.core_ref, bf16[512,256]{1,0:T(8,128)(2,1)S(1)} %collective-permute-done.left_ref, bf16[512,256]{1,0:T(8,128)(2,1)S(1)} %get-tuple-element.16.right_ref, bf16[512,128]{1,0:T(8,128)(2,1)S(1)} %get-tuple-element.17.own_ref), custom_call_target="tpu_custom_call" | custom-call | tf_op jit(solution)/shard_map/other/pallas_call | solution.py:317
  35.5 0.0 copy-start
  35.6 19.3 %all_to_all.11 = bf16[128,8,128]{2,1,0:T(8,128)(2,1)S(1)} all-to-all(bf16[128,8,128]{2,1,0:T(8,128)(2,1)S(1)} %other.1), channel_id=1, replica_groups={{196,0,2,6,8,16,112,136,4,10,14,18,22,24,32,96,114,118,120,128,138,142,..., dimensions={0} | all-to-all | bytes 524288 | tf_op jit(solution)/shard_map/all_to_all | solution.py:263
  54.8 0.0 copy-done
  54.8 1.1 %output.1 = bf16[1024,128]{1,0:T(8,128)(2,1)} custom-call(bf16[1024,128]{1,0:T(8,128)(2,1)S(1)} %bitcast.12, f32[1280,128]{1,0:T(8,128)S(1)} %get-tuple-element.18.gate_ref, bf16[128,128]{1,0:T(8,128)(2,1)S(1)} %copy-done), custom_call_target="tpu_custom_call" | custom-call | tf_op jit(solution)/shard_map/output/pallas_call | solution.py:327
Async XLA Ops:
  32.1 2.8 %collective-permute-start = (bf16[512,256]{1,0:T(8,128)(2,1)S(1)}, bf16[512,256]{1,0:T(8,128)(2,1)S(1)}, u32[]{:S(2)}, u32[]{:S(2)}) collective-permute-start(bf16[512,256]{1,0:T(8,128)(2,1)S(1)} %spread.1.left_ref), channel_id=1, source_target_pairs={{0,1},{1,0},{2,3},{3,2},{4,5},{5,4},{6,7},{7,6},{8,9},{9,8},{10,11... | collective-permute-start | bytes 786440 | tf_op jit(solution)/shard_map/ppermute | solution.py:306
  35.5 19.3 %copy-start = (bf16[128,128]{1,0:T(8,128)(2,1)S(1)}, bf16[128,128]{1,0:T(8,128)(2,1)}, u32[]{:S(2)}) copy-start(bf16[128,128]{1,0:T(8,128)(2,1)} %w_ref.1) | copy-start | bytes 98308

commit v7 on v6

--- a/solution.py
+++ b/solution.py
@@ -10,7 +10,7 @@
 
 EPSILON = 1e-05
 AXES = ("xh", "z", "xl", "y", "core")
-ROOT = (1, 4, 0, 2)
+ROOT = (1, 5, 0, 2)
 
 
 def hops(p, q):
@@ -152,7 +152,7 @@
     return a + xh * (c - a) + core * ((b - a) + xh * (a - b - c + d))
 
 
-def pieces(mixed_ref, store):
+def pieces(mixed_ref, store, static=False):
     def step(xl, carry):
         for y in range(4):
             for g in range(2):
@@ -163,7 +163,11 @@
                 store(xl, y, g, swap_groups(v))
         return carry
 
-    lax.fori_loop(0, 2, step, 0)
+    if static:
+        for t in range(2):
+            step(t, 0)
+    else:
+        lax.fori_loop(0, 2, step, 0)
 
 
 def own_kernel(
@@ -196,7 +200,7 @@
             out_ref[member(xl, y, core, (g, c))] = own_ref[pl.ds(start, 8), :]
             out_ref[member(xl, y, 1 - core, (g, c))] = v[c].astype(BF16)
 
-    pieces(mixed_ref, store)
+    pieces(mixed_ref, store, True)
 
 
 def output_kernel(recv_ref, gate_ref, w_ref, out_hbm, scr_ref, out_ref, sem):

time: 56.2 us -> 55.4 us (0.986)
  no operation moved by 1% of the time
where the time goes in v7:
time: 55.4 us; the launch traced here: 55 us
  blocking collectives  48.4 us (87%)
  Pallas kernels  5.24 us (9%)
  starting transfers between devices  1.28 us (2%)
    all_to_all x2, blocking collectives, exchange(): lax.all_to_all(x, AXES, 0, 0, axis_index_groups=chip_groups(), tiled=True)  48.4 us
    pallas_call x1, Pallas kernels, local(): pl.pallas_call(project_kernel, out_shape=(shape((2048, 128), BF16), shape...  2.09 us
    ppermute x1, starting transfers between devices, local(): other = lax.ppermute(left, 'core', [(0, 1), (1, 0)])  1.28 us
    pallas_call x1, Pallas kernels, local(): pl.pallas_call(own_kernel, out_shape=(shape((512, 256), BF16), shape((512...  1.14 us
    pallas_call x1, Pallas kernels, local(): pl.pallas_call(output_kernel, out_shape=shape((1024, 128), BF16), in_spec...  1.13 us
  transfers between devices with their start and end apart: 1, of which 0 were waited for; matrix products, arithmetic and copies ran while one was open for 0% of the time, Pallas kernels for 2%

profile of v7, /device:TPU:1, one launch (start us, length us, event | category | flops | bytes accessed | tf_op | source)
XLA Modules:
  0.0 55.0 jit_solution(4732349283250052985)
XLA Ops:
  0.0 2.1 %project.1 = (bf16[2048,128]{1,0:T(8,128)(2,1)S(1)}, bf16[1024,128]{1,0:T(8,128)(2,1)S(1)}, f32[16,128]{1,0:T(8,128)S(1)}, bf16[128,128]{1,0:T(8,128)(2,1)S(1)}) custom-call(bf16[1024,128]{1,0:T(8,128)(2,1)} %bitcast.14, f32[1,128]{1,0:T(1,128)} %bitcast.15, f32[1,128]{1,0:T(1,128)} %bitcast.16, bf16[128,640]{1,0:T(8,128)(2,1)} %w_hbm.1, f32[1,128]{1,0:T(1,128)} %bitcast.17, ...), custom_call_target="tpu_custom_call" | custom-call | tf_op jit(solution)/shard_map/project/pallas_call | solution.py:274
  2.1 29.0 %all_to_all.10 = bf16[128,16,128]{2,1,0:T(8,128)(2,1)S(1)} all-to-all(bf16[128,16,128]{2,1,0:T(8,128)(2,1)S(1)} %bitcast.13), channel_id=1, replica_groups={{212,16,0,18,22,24,32,152,2,6,8,20,26,30,34,38,40,48,112,136,144,154,15..., dimensions={0} | all-to-all | bytes 1048576 | tf_op jit(solution)/shard_map/all_to_all | solution.py:267
  31.1 0.4 spread.1.left_ref
  31.5 1.3 %collective-permute-start = (bf16[512,256]{1,0:T(8,128)(2,1)S(1)}, bf16[512,256]{1,0:T(8,128)(2,1)S(1)}, u32[]{:S(2)}, u32[]{:S(2)}) collective-permute-start(bf16[512,256]{1,0:T(8,128)(2,1)S(1)} %spread.1.left_ref), channel_id=1, source_target_pairs={{0,1},{1,0},{2,3},{3,2},{4,5},{5,4},{6,7},{7,6},{8,9},{9,8},{10,11... | collective-permute-start | bytes 786440 | tf_op jit(solution)/shard_map/ppermute | solution.py:310
  32.8 1.1 %own.1 = (bf16[512,256]{1,0:T(8,128)(2,1)S(1)}, bf16[512,128]{1,0:T(8,128)(2,1)S(1)}, f32[1280,128]{1,0:T(8,128)S(1)}) custom-call(bf16[2048,128]{1,0:T(8,128)(2,1)S(1)} %bitcast.11, bf16[512,256]{1,0:T(8,128)(2,1)S(1)} %spread.1.left_ref, bf16[1024,128]{1,0:T(8,128)(2,1)S(1)} %get-tuple-element.13.normed_ref, f32[16,128]{1,0:T(8,128)S(1)} %get-tuple-element.14.aux_ref, ...), custom_call_target="tpu_custom_call" | custom-call | flops 67108864 | bytes 1048576 | tf_op jit(solution)/shard_map/own/pallas_call | solution.py:311
  33.9 0.0 collective-permute-done.left_ref
  34.0 0.5 other.1
  34.4 0.0 copy-start
  34.4 19.4 %all_to_all.11 = bf16[128,8,128]{2,1,0:T(8,128)(2,1)S(1)} all-to-all(bf16[128,8,128]{2,1,0:T(8,128)(2,1)S(1)} %other.1), channel_id=1, replica_groups={{212,16,0,18,22,24,32,152,2,6,8,20,26,30,34,38,40,48,112,136,144,154,15..., dimensions={0} | all-to-all | bytes 524288 | tf_op jit(solution)/shard_map/all_to_all | solution.py:267
  53.8 0.0 copy-done
  53.9 1.1 %output.1 = bf16[1024,128]{1,0:T(8,128)(2,1)} custom-call(bf16[1024,128]{1,0:T(8,128)(2,1)S(1)} %bitcast.12, f32[1280,128]{1,0:T(8,128)S(1)} %get-tuple-element.18.gate_ref, bf16[128,128]{1,0:T(8,128)(2,1)S(1)} %copy-done), custom_call_target="tpu_custom_call" | custom-call | tf_op jit(solution)/shard_map/output/pallas_call | solution.py:331
Async XLA Ops:
  31.5 2.4 %collective-permute-start = (bf16[512,256]{1,0:T(8,128)(2,1)S(1)}, bf16[512,256]{1,0:T(8,128)(2,1)S(1)}, u32[]{:S(2)}, u32[]{:S(2)}) collective-permute-start(bf16[512,256]{1,0:T(8,128)(2,1)S(1)} %spread.1.left_ref), channel_id=1, source_target_pairs={{0,1},{1,0},{2,3},{3,2},{4,5},{5,4},{6,7},{7,6},{8,9},{9,8},{10,11... | collective-permute-start | bytes 786440 | tf_op jit(solution)/shard_map/ppermute | solution.py:310
  34.4 19.4 %copy-start = (bf16[128,128]{1,0:T(8,128)(2,1)S(1)}, bf16[128,128]{1,0:T(8,128)(2,1)}, u32[]{:S(2)}) copy-start(bf16[128,128]{1,0:T(8,128)(2,1)} %w_ref.1) | copy-start | bytes 98308

commit v8 on v7

--- a/solution.py
+++ b/solution.py
@@ -50,28 +50,23 @@
 
 
 def project_kernel(
-    pair_hbm, gain_hbm, shift_hbm, w_hbm, gain_out_hbm, shift_out_hbm,
-    msg_ref, normed_ref, aux_ref, w_gate_ref,
+    pair_hbm, gain_hbm, shift_hbm, w_hbm, msg_ref, normed_ref,
     pair_ref, w_ref, rows_ref, scr_ref, sem,
 ):
     def pair_copy(t):
         rows = pl.ds(t * 512, 512)
-        return pltpu.make_async_copy(pair_hbm.at[rows], pair_ref.at[rows], sem.at[6 + t])
+        return pltpu.make_async_copy(pair_hbm.at[rows], pair_ref.at[rows], sem.at[3 + t])
 
     small = [
         pltpu.make_async_copy(ref, rows_ref.at[pl.ds(t * 8, 1)], sem.at[t])
-        for t, ref in enumerate((gain_hbm, shift_hbm, gain_out_hbm, shift_out_hbm))
+        for t, ref in enumerate((gain_hbm, shift_hbm))
     ]
-    w_copy = pltpu.make_async_copy(w_hbm.at[:, pl.ds(0, 512)], w_ref, sem.at[4])
-    w_gate_copy = pltpu.make_async_copy(w_hbm.at[:, pl.ds(512, 128)], w_gate_ref, sem.at[5])
+    w_copy = pltpu.make_async_copy(w_hbm.at[:, pl.ds(0, 512)], w_ref, sem.at[2])
+    pair_copy(0).start()
     small[0].start()
     small[1].start()
-    pair_copy(0).start()
+    w_copy.start()
     pair_copy(1).start()
-    w_copy.start()
-    small[2].start()
-    small[3].start()
-    w_gate_copy.start()
     small[0].wait()
     small[1].wait()
     gain = rows_ref[0:1, :]
@@ -115,11 +110,6 @@
         return carry
 
     lax.fori_loop(0, 4, pack, 0)
-    small[2].wait()
-    small[3].wait()
-    aux_ref[0:1, :] = rows_ref[16:17, :]
-    aux_ref[8:9, :] = rows_ref[24:25, :]
-    w_gate_copy.wait()
 
 
 def spread_kernel(offset, recv_ref, out_ref):
@@ -171,22 +161,33 @@
 
 
 def own_kernel(
-    recv_ref, left_ref, normed_ref, aux_ref, w_gate_ref, right_ref, out_ref, gate_ref, mixed_ref
+    recv_ref, left_ref, normed_ref, gain_hbm, shift_hbm, w_hbm,
+    right_ref, out_ref, gate_ref,
+    mixed_ref, rows_ref, w_gate_ref, sem,
 ):
+    copies = [
+        pltpu.make_async_copy(w_hbm.at[:, pl.ds(512, 128)], w_gate_ref, sem.at[0]),
+        pltpu.make_async_copy(gain_hbm, rows_ref.at[pl.ds(0, 1)], sem.at[1]),
+        pltpu.make_async_copy(shift_hbm, rows_ref.at[pl.ds(8, 1)], sem.at[2]),
+    ]
+    for copy in copies:
+        copy.start()
     spread_kernel(8, recv_ref, right_ref)
     multiply(left_ref, right_ref, mixed_ref)
+
+    def store(xl, y, g, v):
+        start = pl.multiple_of(((xl * 4 + y) * 2 + g) * 32, 32)
+        out_ref[pl.ds(start, 32), :] = jnp.concatenate(v, axis=0).astype(BF16)
+
+    pieces(mixed_ref, store, True)
+    for copy in copies:
+        copy.wait()
     gate_ref[0:1024, :] = jax.nn.sigmoid(
         jnp.dot(normed_ref[...], w_gate_ref[...], preferred_element_type=F32)
     )
-
-    def store(xl, y, g, v):
-        start = pl.multiple_of(((xl * 4 + y) * 2 + g) * 32, 32)
-        out_ref[pl.ds(start, 32), :] = jnp.concatenate(v, axis=0).astype(BF16)
-
-    pieces(mixed_ref, store)
     for k in range(2):
         gate_ref[1024 + 128 * k : 1152 + 128 * k, :] = jnp.transpose(
-            jnp.broadcast_to(aux_ref[8 * k : 8 * k + 1, :], (128, 128))
+            jnp.broadcast_to(rows_ref[8 * k : 8 * k + 1, :], (128, 128))
         )
 
 
@@ -271,22 +272,17 @@
     core = lax.axis_index("core").astype(jnp.int32).reshape(1)
     shape = jax.ShapeDtypeStruct
     stay = functools.partial(pltpu.with_memory_space_constraint, memory_space=pltpu.HBM)
-    msg, normed, aux, w_gate = pl.pallas_call(
+    msg, normed = pl.pallas_call(
         project_kernel,
-        out_shape=(
-            shape((2048, 128), BF16),
-            shape((1024, 128), BF16),
-            shape((16, 128), F32),
-            shape((128, 128), BF16),
-        ),
-        in_specs=[HBM] * 6,
-        out_specs=(VMEM,) * 4,
+        out_shape=(shape((2048, 128), BF16), shape((1024, 128), BF16)),
+        in_specs=[HBM] * 4,
+        out_specs=(VMEM,) * 2,
         scratch_shapes=[
             pltpu.VMEM((1024, 128), BF16),
             pltpu.VMEM((128, 512), BF16),
-            pltpu.VMEM((32, 128), F32),
+            pltpu.VMEM((16, 128), F32),
             pltpu.VMEM((2048, 128), F32),
-            pltpu.SemaphoreType.DMA((8,)),
+            pltpu.SemaphoreType.DMA((5,)),
         ],
         compiler_params=SMALL,
         name="project",
@@ -295,8 +291,6 @@
         stay(norm_in.reshape(1, 128)),
         stay(shift_in.reshape(1, 128)),
         stay(in_weight),
-        stay(norm_out.reshape(1, 128)),
-        stay(shift_out.reshape(1, 128)),
     )
     recv = exchange(msg.reshape(128, 16, 128)).reshape(2048, 128)
     left = pl.pallas_call(
@@ -311,13 +305,25 @@
     right, own, gate = pl.pallas_call(
         own_kernel,
         out_shape=(shape((512, 256), BF16), shape((512, 128), BF16), shape((1280, 128), F32)),
-        in_specs=[VMEM] * 5,
+        in_specs=[VMEM] * 3 + [HBM] * 3,
         out_specs=(VMEM,) * 3,
-        scratch_shapes=[pltpu.VMEM((256, 256), F32)],
+        scratch_shapes=[
+            pltpu.VMEM((256, 256), F32),
+            pltpu.VMEM((16, 128), F32),
+            pltpu.VMEM((128, 128), BF16),
+            pltpu.SemaphoreType.DMA((3,)),
+        ],
         compiler_params=SMALL,
         name="own",
         cost_estimate=pl.CostEstimate(flops=1 << 26, bytes_accessed=1 << 20, transcendentals=0),
-    )(recv, left, normed, aux, w_gate)
+    )(
+        recv,
+        left,
+        normed,
+        stay(norm_out.reshape(1, 128)),
+        stay(shift_out.reshape(1, 128)),
+        stay(in_weight),
+    )
     back = pl.pallas_call(
         other_kernel,
         out_shape=shape((128, 8, 128), BF16),

time: 55.4 us -> 55.4 us (level)
  no operation moved by 1% of the time
where the time goes in v8:
time: 55.4 us; the launch traced here: 55 us
  blocking collectives  48.4 us (87%)
  Pallas kernels  5.22 us (9%)
  starting transfers between devices  1.28 us (2%)
    all_to_all x2, blocking collectives, exchange(): lax.all_to_all(x, AXES, 0, 0, axis_index_groups=chip_groups(), tiled=True)  48.4 us
    pallas_call x1, Pallas kernels, local(): pl.pallas_call(project_kernel, out_shape=(shape((2048, 128), BF16), shape...  2.02 us
    ppermute x1, starting transfers between devices, local(): other = lax.ppermute(left, 'core', [(0, 1), (1, 0)])  1.28 us
    pallas_call x1, Pallas kernels, local(): pl.pallas_call(own_kernel, out_shape=(shape((512, 256), BF16), shape((512...  1.18 us
    pallas_call x1, Pallas kernels, local(): pl.pallas_call(output_kernel, out_shape=shape((1024, 128), BF16), in_spec...  1.13 us
  transfers between devices with their start and end apart: 1, of which 0 were waited for; matrix products, arithmetic and copies ran while one was open for 0% of the time, Pallas kernels for 2%

profile of v8, /device:TPU:1, one launch (start us, length us, event | category | flops | bytes accessed | tf_op | source)
XLA Modules:
  0.0 55.0 jit_solution(16998596977677736896)
XLA Ops:
  0.0 2.0 %project.1 = (bf16[2048,128]{1,0:T(8,128)(2,1)S(1)}, bf16[1024,128]{1,0:T(8,128)(2,1)S(1)}) custom-call(bf16[1024,128]{1,0:T(8,128)(2,1)} %bitcast.14, f32[1,128]{1,0:T(1,128)} %bitcast.15, f32[1,128]{1,0:T(1,128)} %bitcast.16, bf16[128,640]{1,0:T(8,128)(2,1)} %w_hbm.3), custom_call_target="tpu_custom_call" | custom-call | tf_op jit(solution)/shard_map/project/pallas_call | solution.py:275
  2.0 29.0 %all_to_all.10 = bf16[128,16,128]{2,1,0:T(8,128)(2,1)S(1)} all-to-all(bf16[128,16,128]{2,1,0:T(8,128)(2,1)S(1)} %bitcast.13), channel_id=1, replica_groups={{212,16,0,18,22,24,32,152,2,6,8,20,26,30,34,38,40,48,112,136,144,154,15..., dimensions={0} | all-to-all | bytes 1048576 | tf_op jit(solution)/shard_map/all_to_all | solution.py:268
  31.0 0.4 spread.1.left_ref
  31.4 1.3 %collective-permute-start = (bf16[512,256]{1,0:T(8,128)(2,1)S(1)}, bf16[512,256]{1,0:T(8,128)(2,1)S(1)}, u32[]{:S(2)}, u32[]{:S(2)}) collective-permute-start(bf16[512,256]{1,0:T(8,128)(2,1)S(1)} %spread.1.left_ref), channel_id=1, source_target_pairs={{0,1},{1,0},{2,3},{3,2},{4,5},{5,4},{6,7},{7,6},{8,9},{9,8},{10,11... | collective-permute-start | bytes 786440 | tf_op jit(solution)/shard_map/ppermute | solution.py:304
  32.7 1.2 %own.1 = (bf16[512,256]{1,0:T(8,128)(2,1)S(1)}, bf16[512,128]{1,0:T(8,128)(2,1)S(1)}, f32[1280,128]{1,0:T(8,128)S(1)}) custom-call(bf16[2048,128]{1,0:T(8,128)(2,1)S(1)} %bitcast.11, bf16[512,256]{1,0:T(8,128)(2,1)S(1)} %spread.1.left_ref, bf16[1024,128]{1,0:T(8,128)(2,1)S(1)} %get-tuple-element.11.normed_ref, f32[1,128]{1,0:T(1,128)} %bitcast.17, ...), custom_call_target="tpu_custom_call" | custom-call | flops 67108864 | bytes 1048576 | tf_op jit(solution)/shard_map/own/pallas_call | solution.py:305
  33.9 0.0 collective-permute-done.left_ref
  33.9 0.5 other.1
  34.4 0.0 copy-start
  34.4 19.4 %all_to_all.11 = bf16[128,8,128]{2,1,0:T(8,128)(2,1)S(1)} all-to-all(bf16[128,8,128]{2,1,0:T(8,128)(2,1)S(1)} %other.1), channel_id=1, replica_groups={{212,16,0,18,22,24,32,152,2,6,8,20,26,30,34,38,40,48,112,136,144,154,15..., dimensions={0} | all-to-all | bytes 524288 | tf_op jit(solution)/shard_map/all_to_all | solution.py:268
  53.8 0.0 copy-done
  53.8 1.1 %output.1 = bf16[1024,128]{1,0:T(8,128)(2,1)} custom-call(bf16[1024,128]{1,0:T(8,128)(2,1)S(1)} %bitcast.12, f32[1280,128]{1,0:T(8,128)S(1)} %get-tuple-element.14.gate_ref, bf16[128,128]{1,0:T(8,128)(2,1)S(1)} %copy-done), custom_call_target="tpu_custom_call" | custom-call | tf_op jit(solution)/shard_map/output/pallas_call | solution.py:337
Async XLA Ops:
  31.4 2.5 %collective-permute-start = (bf16[512,256]{1,0:T(8,128)(2,1)S(1)}, bf16[512,256]{1,0:T(8,128)(2,1)S(1)}, u32[]{:S(2)}, u32[]{:S(2)}) collective-permute-start(bf16[512,256]{1,0:T(8,128)(2,1)S(1)} %spread.1.left_ref), channel_id=1, source_target_pairs={{0,1},{1,0},{2,3},{3,2},{4,5},{5,4},{6,7},{7,6},{8,9},{9,8},{10,11... | collective-permute-start | bytes 786440 | tf_op jit(solution)/shard_map/ppermute | solution.py:304
  34.4 19.5 %copy-start = (bf16[128,128]{1,0:T(8,128)(2,1)S(1)}, bf16[128,128]{1,0:T(8,128)(2,1)}, u32[]{:S(2)}) copy-start(bf16[128,128]{1,0:T(8,128)(2,1)} %w_ref.1) | copy-start | bytes 98308

commit v9 on v7

--- a/solution.py
+++ b/solution.py
@@ -64,11 +64,11 @@
     ]
     w_copy = pltpu.make_async_copy(w_hbm.at[:, pl.ds(0, 512)], w_ref, sem.at[4])
     w_gate_copy = pltpu.make_async_copy(w_hbm.at[:, pl.ds(512, 128)], w_gate_ref, sem.at[5])
+    pair_copy(0).start()
     small[0].start()
     small[1].start()
-    pair_copy(0).start()
+    w_copy.start()
     pair_copy(1).start()
-    w_copy.start()
     small[2].start()
     small[3].start()
     w_gate_copy.start()
@@ -183,7 +183,7 @@
         start = pl.multiple_of(((xl * 4 + y) * 2 + g) * 32, 32)
         out_ref[pl.ds(start, 32), :] = jnp.concatenate(v, axis=0).astype(BF16)
 
-    pieces(mixed_ref, store)
+    pieces(mixed_ref, store, True)
     for k in range(2):
         gate_ref[1024 + 128 * k : 1152 + 128 * k, :] = jnp.transpose(
             jnp.broadcast_to(aux_ref[8 * k : 8 * k + 1, :], (128, 128))

time: 55.4 us -> 55.4 us (level)
  transfers between devices with their start and end apart: 1 -> 1, of which waited for: 0 -> 1; matrix products, arithmetic and copies ran while one was open for 0% -> 0% of each run, Pallas kernels for 2% -> 2%
where the time goes in v9:
time: 55.4 us; the launch traced here: 55 us
  blocking collectives  48.4 us (87%)
  Pallas kernels  4.99 us (9%)
  starting transfers between devices  1.28 us (2%)
    all_to_all x2, blocking collectives, exchange(): lax.all_to_all(x, AXES, 0, 0, axis_index_groups=chip_groups(), tiled=True)  48.4 us
    pallas_call x1, Pallas kernels, local(): pl.pallas_call(project_kernel, out_shape=(shape((2048, 128), BF16), shape...  2.05 us
    ppermute x1, starting transfers between devices, local(): other = lax.ppermute(left, 'core', [(0, 1), (1, 0)])  1.28 us
    pallas_call x1, Pallas kernels, local(): pl.pallas_call(output_kernel, out_shape=shape((1024, 128), BF16), in_spec...  1.13 us
  transfers between devices with their start and end apart: 1, of which 1 were waited for; matrix products, arithmetic and copies ran while one was open for 0% of the time, Pallas kernels for 2%

profile of v9, /device:TPU:1, one launch (start us, length us, event | category | flops | bytes accessed | tf_op | source)
XLA Modules:
  0.0 55.0 jit_solution(4608080903727956376)
XLA Ops:
  0.0 2.1 %project.1 = (bf16[2048,128]{1,0:T(8,128)(2,1)S(1)}, bf16[1024,128]{1,0:T(8,128)(2,1)S(1)}, f32[16,128]{1,0:T(8,128)S(1)}, bf16[128,128]{1,0:T(8,128)(2,1)S(1)}) custom-call(bf16[1024,128]{1,0:T(8,128)(2,1)} %bitcast.14, f32[1,128]{1,0:T(1,128)} %bitcast.15, f32[1,128]{1,0:T(1,128)} %bitcast.16, bf16[128,640]{1,0:T(8,128)(2,1)} %w_hbm.1, f32[1,128]{1,0:T(1,128)} %bitcast.17, ...), custom_call_target="tpu_custom_call" | custom-call | tf_op jit(solution)/shard_map/project/pallas_call | solution.py:274
  2.1 29.0 %all_to_all.10 = bf16[128,16,128]{2,1,0:T(8,128)(2,1)S(1)} all-to-all(bf16[128,16,128]{2,1,0:T(8,128)(2,1)S(1)} %bitcast.13), channel_id=1, replica_groups={{212,16,0,18,22,24,32,152,2,6,8,20,26,30,34,38,40,48,112,136,144,154,15..., dimensions={0} | all-to-all | bytes 1048576 | tf_op jit(solution)/shard_map/all_to_all | solution.py:267
  31.0 0.4 spread.1.left_ref
  31.5 1.3 %collective-permute-start = (bf16[512,256]{1,0:T(8,128)(2,1)S(1)}, bf16[512,256]{1,0:T(8,128)(2,1)S(1)}, u32[]{:S(2)}, u32[]{:S(2)}) collective-permute-start(bf16[512,256]{1,0:T(8,128)(2,1)S(1)} %spread.1.left_ref), channel_id=1, source_target_pairs={{0,1},{1,0},{2,3},{3,2},{4,5},{5,4},{6,7},{7,6},{8,9},{9,8},{10,11... | collective-permute-start | bytes 786440 | tf_op jit(solution)/shard_map/ppermute | solution.py:310
  32.8 0.9 %own.1 = (bf16[512,256]{1,0:T(8,128)(2,1)S(1)}, bf16[512,128]{1,0:T(8,128)(2,1)S(1)}, f32[1280,128]{1,0:T(8,128)S(1)}) custom-call(bf16[2048,128]{1,0:T(8,128)(2,1)S(1)} %bitcast.11, bf16[512,256]{1,0:T(8,128)(2,1)S(1)} %spread.1.left_ref, bf16[1024,128]{1,0:T(8,128)(2,1)S(1)} %get-tuple-element.13.normed_ref, f32[16,128]{1,0:T(8,128)S(1)} %get-tuple-element.14.aux_ref, ...), custom_call_target="tpu_custom_call" | custom-call | flops 67108864 | bytes 1048576 | tf_op jit(solution)/shard_map/own/pallas_call | solution.py:311
  33.7 0.2 collective-permute-done.left_ref
  33.9 0.4 other.1
  34.4 0.0 copy-start
  34.4 19.4 %all_to_all.11 = bf16[128,8,128]{2,1,0:T(8,128)(2,1)S(1)} all-to-all(bf16[128,8,128]{2,1,0:T(8,128)(2,1)S(1)} %other.1), channel_id=1, replica_groups={{212,16,0,18,22,24,32,152,2,6,8,20,26,30,34,38,40,48,112,136,144,154,15..., dimensions={0} | all-to-all | bytes 524288 | tf_op jit(solution)/shard_map/all_to_all | solution.py:267
  53.8 0.0 copy-done
  53.8 1.1 %output.1 = bf16[1024,128]{1,0:T(8,128)(2,1)} custom-call(bf16[1024,128]{1,0:T(8,128)(2,1)S(1)} %bitcast.12, f32[1280,128]{1,0:T(8,128)S(1)} %get-tuple-element.18.gate_ref, bf16[128,128]{1,0:T(8,128)(2,1)S(1)} %copy-done), custom_call_target="tpu_custom_call" | custom-call | tf_op jit(solution)/shard_map/output/pallas_call | solution.py:331
Async XLA Ops:
  31.5 2.4 %collective-permute-start = (bf16[512,256]{1,0:T(8,128)(2,1)S(1)}, bf16[512,256]{1,0:T(8,128)(2,1)S(1)}, u32[]{:S(2)}, u32[]{:S(2)}) collective-permute-start(bf16[512,256]{1,0:T(8,128)(2,1)S(1)} %spread.1.left_ref), channel_id=1, source_target_pairs={{0,1},{1,0},{2,3},{3,2},{4,5},{5,4},{6,7},{7,6},{8,9},{9,8},{10,11... | collective-permute-start | bytes 786440 | tf_op jit(solution)/shard_map/ppermute | solution.py:310
  34.4 19.4 %copy-start = (bf16[128,128]{1,0:T(8,128)(2,1)S(1)}, bf16[128,128]{1,0:T(8,128)(2,1)}, u32[]{:S(2)}) copy-start(bf16[128,128]{1,0:T(8,128)(2,1)} %w_ref.1) | copy-start | bytes 98308

commit v10 on v7

--- a/solution.py
+++ b/solution.py
@@ -67,8 +67,8 @@
     small[0].start()
     small[1].start()
     pair_copy(0).start()
+    w_copy.start()
     pair_copy(1).start()
-    w_copy.start()
     small[2].start()
     small[3].start()
     w_gate_copy.start()

time: 55.4 us -> 55.4 us (level)
  no operation moved by 1% of the time
where the time goes in v10:
time: 55.4 us; the launch traced here: 55 us
  blocking collectives  48.4 us (87%)
  Pallas kernels  5.24 us (9%)
  starting transfers between devices  1.28 us (2%)
    all_to_all x2, blocking collectives, exchange(): lax.all_to_all(x, AXES, 0, 0, axis_index_groups=chip_groups(), tiled=True)  48.4 us
    pallas_call x1, Pallas kernels, local(): pl.pallas_call(project_kernel, out_shape=(shape((2048, 128), BF16), shape...  2.09 us
    ppermute x1, starting transfers between devices, local(): other = lax.ppermute(left, 'core', [(0, 1), (1, 0)])  1.28 us
    pallas_call x1, Pallas kernels, local(): pl.pallas_call(own_kernel, out_shape=(shape((512, 256), BF16), shape((512...  1.14 us
    pallas_call x1, Pallas kernels, local(): pl.pallas_call(output_kernel, out_shape=shape((1024, 128), BF16), in_spec...  1.13 us
  transfers between devices with their start and end apart: 1, of which 0 were waited for; matrix products, arithmetic and copies ran while one was open for 0% of the time, Pallas kernels for 2%

profile of v10, /device:TPU:1, one launch (start us, length us, event | category | flops | bytes accessed | tf_op | source)
XLA Modules:
  0.0 55.0 jit_solution(4586049223448180914)
XLA Ops:
  0.0 2.1 %project.1 = (bf16[2048,128]{1,0:T(8,128)(2,1)S(1)}, bf16[1024,128]{1,0:T(8,128)(2,1)S(1)}, f32[16,128]{1,0:T(8,128)S(1)}, bf16[128,128]{1,0:T(8,128)(2,1)S(1)}) custom-call(bf16[1024,128]{1,0:T(8,128)(2,1)} %bitcast.14, f32[1,128]{1,0:T(1,128)} %bitcast.15, f32[1,128]{1,0:T(1,128)} %bitcast.16, bf16[128,640]{1,0:T(8,128)(2,1)} %w_hbm.1, f32[1,128]{1,0:T(1,128)} %bitcast.17, ...), custom_call_target="tpu_custom_call" | custom-call | tf_op jit(solution)/shard_map/project/pallas_call | solution.py:274
  2.1 29.0 %all_to_all.10 = bf16[128,16,128]{2,1,0:T(8,128)(2,1)S(1)} all-to-all(bf16[128,16,128]{2,1,0:T(8,128)(2,1)S(1)} %bitcast.13), channel_id=1, replica_groups={{212,16,0,18,22,24,32,152,2,6,8,20,26,30,34,38,40,48,112,136,144,154,15..., dimensions={0} | all-to-all | bytes 1048576 | tf_op jit(solution)/shard_map/all_to_all | solution.py:267
  31.1 0.4 spread.1.left_ref
  31.5 1.3 %collective-permute-start = (bf16[512,256]{1,0:T(8,128)(2,1)S(1)}, bf16[512,256]{1,0:T(8,128)(2,1)S(1)}, u32[]{:S(2)}, u32[]{:S(2)}) collective-permute-start(bf16[512,256]{1,0:T(8,128)(2,1)S(1)} %spread.1.left_ref), channel_id=1, source_target_pairs={{0,1},{1,0},{2,3},{3,2},{4,5},{5,4},{6,7},{7,6},{8,9},{9,8},{10,11... | collective-permute-start | bytes 786440 | tf_op jit(solution)/shard_map/ppermute | solution.py:310
  32.8 1.1 %own.1 = (bf16[512,256]{1,0:T(8,128)(2,1)S(1)}, bf16[512,128]{1,0:T(8,128)(2,1)S(1)}, f32[1280,128]{1,0:T(8,128)S(1)}) custom-call(bf16[2048,128]{1,0:T(8,128)(2,1)S(1)} %bitcast.11, bf16[512,256]{1,0:T(8,128)(2,1)S(1)} %spread.1.left_ref, bf16[1024,128]{1,0:T(8,128)(2,1)S(1)} %get-tuple-element.13.normed_ref, f32[16,128]{1,0:T(8,128)S(1)} %get-tuple-element.14.aux_ref, ...), custom_call_target="tpu_custom_call" | custom-call | flops 67108864 | bytes 1048576 | tf_op jit(solution)/shard_map/own/pallas_call | solution.py:311
  33.9 0.0 collective-permute-done.left_ref
  34.0 0.5 other.1
  34.4 0.0 copy-start
  34.4 19.4 %all_to_all.11 = bf16[128,8,128]{2,1,0:T(8,128)(2,1)S(1)} all-to-all(bf16[128,8,128]{2,1,0:T(8,128)(2,1)S(1)} %other.1), channel_id=1, replica_groups={{212,16,0,18,22,24,32,152,2,6,8,20,26,30,34,38,40,48,112,136,144,154,15..., dimensions={0} | all-to-all | bytes 524288 | tf_op jit(solution)/shard_map/all_to_all | solution.py:267
  53.8 0.0 copy-done
  53.9 1.1 %output.1 = bf16[1024,128]{1,0:T(8,128)(2,1)} custom-call(bf16[1024,128]{1,0:T(8,128)(2,1)S(1)} %bitcast.12, f32[1280,128]{1,0:T(8,128)S(1)} %get-tuple-element.18.gate_ref, bf16[128,128]{1,0:T(8,128)(2,1)S(1)} %copy-done), custom_call_target="tpu_custom_call" | custom-call | tf_op jit(solution)/shard_map/output/pallas_call | solution.py:331
Async XLA Ops:
  31.5 2.4 %collective-permute-start = (bf16[512,256]{1,0:T(8,128)(2,1)S(1)}, bf16[512,256]{1,0:T(8,128)(2,1)S(1)}, u32[]{:S(2)}, u32[]{:S(2)}) collective-permute-start(bf16[512,256]{1,0:T(8,128)(2,1)S(1)} %spread.1.left_ref), channel_id=1, source_target_pairs={{0,1},{1,0},{2,3},{3,2},{4,5},{5,4},{6,7},{7,6},{8,9},{9,8},{10,11... | collective-permute-start | bytes 786440 | tf_op jit(solution)/shard_map/ppermute | solution.py:310
  34.4 19.4 %copy-start = (bf16[128,128]{1,0:T(8,128)(2,1)S(1)}, bf16[128,128]{1,0:T(8,128)(2,1)}, u32[]{:S(2)}) copy-start(bf16[128,128]{1,0:T(8,128)(2,1)} %w_ref.1) | copy-start | bytes 98308

commit v11 on v10

--- a/solution.py
+++ b/solution.py
@@ -64,9 +64,9 @@
     ]
     w_copy = pltpu.make_async_copy(w_hbm.at[:, pl.ds(0, 512)], w_ref, sem.at[4])
     w_gate_copy = pltpu.make_async_copy(w_hbm.at[:, pl.ds(512, 128)], w_gate_ref, sem.at[5])
+    pair_copy(0).start()
     small[0].start()
     small[1].start()
-    pair_copy(0).start()
     w_copy.start()
     pair_copy(1).start()
     small[2].start()
@@ -94,13 +94,13 @@
     norm(1, 0)
 
     def step(t, carry):
-        for u in range(2):
-            n = normed_ref[pl.ds(pl.multiple_of(t * 512 + u * 256, 256), 256), :]
+        for u in range(1):
+            n = normed_ref[pl.ds(t * 512, 512), :]
             p = lax.dot_general(wt, n, (((1,), (1,)), ((), ())), preferred_element_type=F32)
             left = jax.nn.sigmoid(p[0:128]) * p[128:256]
             right = jax.nn.sigmoid(p[256:384]) * p[384:512]
-            for k in range(2):
-                a = t * 4 + u * 2 + k
+            for k in range(4):
+                a = t * 4 + k
                 lanes = slice(k * 128, (k + 1) * 128)
                 scr_ref[pl.ds(a, 128, stride=16), :] = left[:, lanes]
                 scr_ref[pl.ds(8 + a, 128, stride=16), :] = right[:, lanes]

time: 55.4 us -> 55.4 us (level)
  no operation moved by 1% of the time
where the time goes in v11:
time: 55.4 us; the launch traced here: 55 us
  blocking collectives  48.4 us (87%)
  Pallas kernels  5.2 us (9%)
  starting transfers between devices  1.28 us (2%)
    all_to_all x2, blocking collectives, exchange(): lax.all_to_all(x, AXES, 0, 0, axis_index_groups=chip_groups(), tiled=True)  48.4 us
    pallas_call x1, Pallas kernels, local(): pl.pallas_call(project_kernel, out_shape=(shape((2048, 128), BF16), shape...  2.05 us
    ppermute x1, starting transfers between devices, local(): other = lax.ppermute(left, 'core', [(0, 1), (1, 0)])  1.28 us
    pallas_call x1, Pallas kernels, local(): pl.pallas_call(own_kernel, out_shape=(shape((512, 256), BF16), shape((512...  1.14 us
    pallas_call x1, Pallas kernels, local(): pl.pallas_call(output_kernel, out_shape=shape((1024, 128), BF16), in_spec...  1.13 us
  transfers between devices with their start and end apart: 1, of which 0 were waited for; matrix products, arithmetic and copies ran while one was open for 0% of the time, Pallas kernels for 2%

profile of v11, /device:TPU:1, one launch (start us, length us, event | category | flops | bytes accessed | tf_op | source)
XLA Modules:
  0.0 55.0 jit_solution(3669306790845802268)
XLA Ops:
  0.0 2.1 %project.1 = (bf16[2048,128]{1,0:T(8,128)(2,1)S(1)}, bf16[1024,128]{1,0:T(8,128)(2,1)S(1)}, f32[16,128]{1,0:T(8,128)S(1)}, bf16[128,128]{1,0:T(8,128)(2,1)S(1)}) custom-call(bf16[1024,128]{1,0:T(8,128)(2,1)} %bitcast.14, f32[1,128]{1,0:T(1,128)} %bitcast.15, f32[1,128]{1,0:T(1,128)} %bitcast.16, bf16[128,640]{1,0:T(8,128)(2,1)} %w_hbm.1, f32[1,128]{1,0:T(1,128)} %bitcast.17, ...), custom_call_target="tpu_custom_call" | custom-call | tf_op jit(solution)/shard_map/project/pallas_call | solution.py:274
  2.1 29.0 %all_to_all.10 = bf16[128,16,128]{2,1,0:T(8,128)(2,1)S(1)} all-to-all(bf16[128,16,128]{2,1,0:T(8,128)(2,1)S(1)} %bitcast.13), channel_id=1, replica_groups={{212,16,0,18,22,24,32,152,2,6,8,20,26,30,34,38,40,48,112,136,144,154,15..., dimensions={0} | all-to-all | bytes 1048576 | tf_op jit(solution)/shard_map/all_to_all | solution.py:267
  31.0 0.4 spread.1.left_ref
  31.5 1.3 %collective-permute-start = (bf16[512,256]{1,0:T(8,128)(2,1)S(1)}, bf16[512,256]{1,0:T(8,128)(2,1)S(1)}, u32[]{:S(2)}, u32[]{:S(2)}) collective-permute-start(bf16[512,256]{1,0:T(8,128)(2,1)S(1)} %spread.1.left_ref), channel_id=1, source_target_pairs={{0,1},{1,0},{2,3},{3,2},{4,5},{5,4},{6,7},{7,6},{8,9},{9,8},{10,11... | collective-permute-start | bytes 786440 | tf_op jit(solution)/shard_map/ppermute | solution.py:310
  32.8 1.1 %own.1 = (bf16[512,256]{1,0:T(8,128)(2,1)S(1)}, bf16[512,128]{1,0:T(8,128)(2,1)S(1)}, f32[1280,128]{1,0:T(8,128)S(1)}) custom-call(bf16[2048,128]{1,0:T(8,128)(2,1)S(1)} %bitcast.11, bf16[512,256]{1,0:T(8,128)(2,1)S(1)} %spread.1.left_ref, bf16[1024,128]{1,0:T(8,128)(2,1)S(1)} %get-tuple-element.13.normed_ref, f32[16,128]{1,0:T(8,128)S(1)} %get-tuple-element.14.aux_ref, ...), custom_call_target="tpu_custom_call" | custom-call | flops 67108864 | bytes 1048576 | tf_op jit(solution)/shard_map/own/pallas_call | solution.py:311
  33.9 0.0 collective-permute-done.left_ref
  33.9 0.4 other.1
  34.4 0.0 copy-start
  34.4 19.4 %all_to_all.11 = bf16[128,8,128]{2,1,0:T(8,128)(2,1)S(1)} all-to-all(bf16[128,8,128]{2,1,0:T(8,128)(2,1)S(1)} %other.1), channel_id=1, replica_groups={{212,16,0,18,22,24,32,152,2,6,8,20,26,30,34,38,40,48,112,136,144,154,15..., dimensions={0} | all-to-all | bytes 524288 | tf_op jit(solution)/shard_map/all_to_all | solution.py:267
  53.8 0.0 copy-done
  53.8 1.1 %output.1 = bf16[1024,128]{1,0:T(8,128)(2,1)} custom-call(bf16[1024,128]{1,0:T(8,128)(2,1)S(1)} %bitcast.12, f32[1280,128]{1,0:T(8,128)S(1)} %get-tuple-element.18.gate_ref, bf16[128,128]{1,0:T(8,128)(2,1)S(1)} %copy-done), custom_call_target="tpu_custom_call" | custom-call | tf_op jit(solution)/shard_map/output/pallas_call | solution.py:331
Async XLA Ops:
  31.5 2.4 %collective-permute-start = (bf16[512,256]{1,0:T(8,128)(2,1)S(1)}, bf16[512,256]{1,0:T(8,128)(2,1)S(1)}, u32[]{:S(2)}, u32[]{:S(2)}) collective-permute-start(bf16[512,256]{1,0:T(8,128)(2,1)S(1)} %spread.1.left_ref), channel_id=1, source_target_pairs={{0,1},{1,0},{2,3},{3,2},{4,5},{5,4},{6,7},{7,6},{8,9},{9,8},{10,11... | collective-permute-start | bytes 786440 | tf_op jit(solution)/shard_map/ppermute | solution.py:310
  34.4 19.4 %copy-start = (bf16[128,128]{1,0:T(8,128)(2,1)S(1)}, bf16[128,128]{1,0:T(8,128)(2,1)}, u32[]{:S(2)}) copy-start(bf16[128,128]{1,0:T(8,128)(2,1)} %w_ref.1) | copy-start | bytes 98308
